TPU v7x, 128 devices: a whole 4x4x4 slice. The times are simulated.
128 devices in a mesh: row: 16 (over x, y), col: 8 (over z, core).
Axes of the slice: x: 4, y: 4, z: 4, core: 2. Of those that a mesh axis runs over, the one named last changes fastest.
Arguments:
- design: bfloat16 [16384, 6144], P(('row', 'col')), may hold values from -0.046875 to 0.046875
- observations: float32 [16384], P(('row', 'col')), may hold values from -6 to 6
- gaps: int32 [16384], P(('row', 'col')), may hold values 0 or 1
- noise_var: float32 [16384], P(('row', 'col')), may hold values from 0.25 to 4
- arc_lengths: int32 [128, 4], P(('row', 'col')), may hold values from 1 to 64, 128 in all within a row
- arc_amp: float32 [128, 4], P(('row', 'col')), may hold values from 0.2 to 2
- arc_decay: float32 [128, 4], P(('row', 'col')), may hold values from 0.3 to 0.95
- plan: int32 [128], P(('row', 'col')), may hold values from 0 to 127, each once
- tile_map: int32 [48], replicated, may hold values from 0 to 47, each once
Outputs:
- gram: float32 [6144, 6144], P('row', 'col')
- normal_rhs: float32 [6144], P('row')
- balanced_obs: float32 [128, 128], P(('row', 'col'))
Inputs may be any that keep to these rules, and one draw needn't show every extreme that they name: `plan`: a permutation of the blocks. `tile_map`: a permutation of the tiles. `arc_lengths`: each block's arc lengths sum to 128; some arc has 64 rows.
All inputs are finite; a program needn't handle non-finite values. No bound on the sum of `gaps` on one device may be relied on, other than what follows from the above.
Results may differ from a plain program's by a relative error of at most 0.004.
Values may be sent and summed in bfloat16 or wider, within the bound.
A program may use at most 192 MiB of HBM per device.

v0:
```python
import jax
import jax.numpy as jnp
from jax import lax
from jax.sharding import PartitionSpec as P


def whiten(block, obs_rows, live_rows, noise_rows, lengths, amplitude, decay):
    block_rows = block.shape[0]
    arc_count = lengths.shape[0]
    position = jnp.arange(block_rows, dtype=jnp.int32)
    arc_ends = jnp.cumsum(lengths)
    arc_id = jnp.sum((arc_ends[None, :] <= position[:, None]).astype(jnp.int32), axis=1)
    member = (arc_id[:, None] == jnp.arange(arc_count, dtype=jnp.int32)[None, :]).astype(
        jnp.float32
    )
    row_amp = jnp.sum(member * amplitude[None, :], axis=1)
    row_rate = jnp.sum(member * jnp.log(decay)[None, :], axis=1)
    same_arc = (arc_id[:, None] == arc_id[None, :]).astype(jnp.float32)
    row_lag = jnp.abs(position[:, None] - position[None, :]).astype(jnp.float32)
    kernel = (
        row_amp[:, None]
        * jnp.exp(row_lag * row_rate[:, None])
        * same_arc
        * live_rows[:, None]
        * live_rows[None, :]
    )
    covariance = kernel + jnp.diag(noise_rows)
    factor = jnp.linalg.cholesky(covariance)
    solved = lax.linalg.triangular_solve(
        factor, block.astype(jnp.float32) * live_rows[:, None], left_side=True, lower=True
    )
    solved_obs = lax.linalg.triangular_solve(
        factor, (obs_rows * live_rows)[:, None], left_side=True, lower=True
    )
    return (solved.astype(jnp.bfloat16), solved_obs[:, 0])


def on_device(
    design, observations, gaps, noise_var, arc_lengths, arc_amp, arc_decay, plan, tile_map
):
    block_count = arc_lengths.shape[0]
    block_rows = design.shape[0] // block_count
    columns = design.shape[1]
    tile_count = tile_map.shape[0]
    tile_size = columns // tile_count
    local_rows = block_count * block_rows
    live_rows = gaps.astype(jnp.float32)
    white, white_obs = jax.vmap(whiten)(
        design.reshape(block_count, block_rows, columns),
        observations.reshape(block_count, block_rows),
        live_rows.reshape(block_count, block_rows),
        noise_var.reshape(block_count, block_rows),
        arc_lengths,
        arc_amp,
        arc_decay,
    )
    slotted = jnp.take(white.reshape(local_rows, tile_count, tile_size), tile_map, axis=1)
    obs_every = lax.all_gather(white_obs.reshape(local_rows), ("row", "col"), axis=0, tiled=True)
    total_rows = obs_every.shape[0]
    row_devices = lax.axis_size("row")
    col_devices = lax.axis_size("col")
    row_tiles = tile_count // row_devices
    col_tiles = tile_count // col_devices
    own_rows = lax.all_to_all(slotted, "row", split_axis=1, concat_axis=0, tiled=True)
    row_panel = lax.all_gather(own_rows, "col", axis=0, tiled=True)
    row_panel = row_panel.reshape(col_devices, row_devices, local_rows, row_tiles * tile_size)
    row_panel = jnp.swapaxes(row_panel, 0, 1).reshape(total_rows, row_tiles * tile_size)
    own_cols = lax.all_to_all(slotted, "col", split_axis=1, concat_axis=0, tiled=True)
    shard_piece = lax.all_gather(own_cols, "row", axis=0, tiled=True)
    piece_rows = shard_piece.shape[0]
    flat_piece = shard_piece.reshape(piece_rows, col_tiles * tile_size)
    gram = lax.dot_general(
        row_panel, flat_piece, (((0,), (0,)), ((), ())), preferred_element_type=jnp.float32
    )
    obs_half = obs_every.astype(jnp.bfloat16)
    normal_rhs = jnp.dot(obs_half, row_panel, preferred_element_type=jnp.float32)
    balanced_obs = jnp.take(obs_every.reshape(-1, block_rows), plan, axis=0)
    return (gram, normal_rhs, balanced_obs)


def solution(mesh):
    placed = (
        P(("row", "col"), None),
        P(("row", "col")),
        P(("row", "col")),
        P(("row", "col")),
        P(("row", "col"), None),
        P(("row", "col"), None),
        P(("row", "col"), None),
        P(("row", "col")),
        P(),
    )
    return jax.shard_map(
        on_device,
        mesh=mesh,
        in_specs=placed,
        out_specs=(P("row", "col"), P("row"), P(("row", "col"), None)),
        check_vma=False,
    )
```

profile of v0, /device:TPU:1, one launch (start us, length us, event | category | flops | bytes accessed | tf_op | source)
XLA Modules:
  0.0 359.8 jit_solution(17996068775224611112)
XLA Ops:
  7.2 0.7 compare_and_fusion
  9.2 0.8 reduce_window_sum.11
  10.1 0.7 log_bitcast_fusion
  10.8 0.7 select_reduce_fusion.2
  11.5 0.8 select_add_fusion
  12.4 0.8 fusion.9
  13.2 11.7 %custom-call.9 = f32[1,128,128]{2,1,0:T(8,128)S(1)} custom-call(f32[1,128,128]{2,1,0:T(8,128)S(1)} %fusion.9), custom_call_target="Cholesky" | custom-call | tf_op jit(solution)/shard_map/vmap(jit(cholesky))/cholesky | solution.py:28
  25.6 0.7 fusion.6
  26.3 9.8 %custom-call.10 = f32[1,1,128,128]{2,3,1,0:T(8,128)S(1)} custom-call(f32[1,1,128,128]{3,2,1,0:T(8,128)S(1)} %fusion.6), custom_call_target="InvertDiagBlocksLowerTriangular" | custom-call | tf_op jit(solution)/shard_map/vmap()/triangular_solve | solution.py:29
  36.1 4.3 %fusion.3 = bf16[16,48,8,128]{3,2,1,0:T(8,128)(2,1)S(1)} fusion(bf16[128,6144]{1,0:T(8,128)(2,1)} %param.9, f32[128]{0:T(128)S(1)} %convert_element_type.39, f32[1,1,128,128]{2,3,1,0:T(8,128)S(1)} %custom-call.10), kind=kOutput, calls=%fused_computation.7 | convolution fusion | flops 1210318848 | bytes 3211776 | tf_op jit(solution)/shard_map/vmap()/triangular_solve | solution.py:29
  40.9 0.9 gather_fusion
  42.0 28.9 %all_to_all.36 = bf16[128,48,128]{2,0,1:T(8,128)(2,1)S(1)} all-to-all(bf16[128,48,128]{2,0,1:T(8,128)(2,1)S(1)} %select_bitcast_fusion), channel_id=1, replica_groups=mesh['row'=16,'col'=8] {'row'}, dimensions={1} | all-to-all | bytes 3145728 | tf_op jit(solution)/shard_map/all_to_all | solution.py:64
  70.9 1.2 copy.30
  72.2 39.8 %all_to_all.37 = bf16[128,48,128]{2,0,1:T(8,128)(2,1)S(1)} all-to-all(bf16[128,48,128]{2,0,1:T(8,128)(2,1)S(1)} %select_bitcast_fusion), channel_id=1, replica_groups=mesh['row'=16,'col'=8] {'col'}, dimensions={1} | all-to-all | bytes 3145728 | tf_op jit(solution)/shard_map/all_to_all | solution.py:68
  112.0 1.3 copy.33
  114.1 29.7 %all-gather = f32[128,1,128]{2,1,0:T(1,128)S(1)} all-gather(f32[1,1,128]{2,1,0:T(1,128)S(1)} %convolution_bitcast_fusion), channel_id=1, replica_groups=mesh['row'=16,'col'=8] {'row','col'}, dimensions={0}, use_global_device_ids=true | all-gather | bytes 66048 | tf_op jit(solution)/shard_map/all_gather | solution.py:58
  144.4 9.0 %all-gather.4.cloned.1.call-done = bf16[16384,3,128]{2,0,1:T(8,128)(2,1)} async-done(((bf16[2048,3,128]{2,0,1:T(8,128)(2,1)}), bf16[16384,3,128]{2,0,1:T(8,128)(2,1)}) %all-gather.4.cloned.1.call-update) | async-done | bytes 12582928 | tf_op jit(solution)/shard_map/all_gather | solution.py:65
  153.4 16.6 %copy.31 = bf16[16384,3,128]{0,2,1:T(8,128)(2,1)} copy(bf16[16384,3,128]{2,0,1:T(8,128)(2,1)} %all-gather.4.cloned.1.call-done) | data formatting | bytes 25165824 | tf_op jit(solution)/shard_map/all_gather | solution.py:65
  170.0 11.7 %copy.37 = bf16[48,8,128,128]{3,2,1,0:T(8,128)(2,1)} copy(bf16[48,8,128,128]{3,1,2,0:T(8,128)(2,1)} %bitcast.60) | data formatting | bytes 25165824
  181.7 17.5 %copy.32 = bf16[16,8,128,384]{3,2,1,0:T(8,128)(2,1)} copy(bf16[16,8,128,384]{2,0,1,3:T(8,128)(2,1)} %bitcast.61) | data formatting | bytes 25165824 | tf_op jit(solution)/shard_map/transpose | solution.py:67
  199.2 9.0 %convolution_reduce_fusion = f32[384]{0:T(512)} fusion(bf16[16384,1]{0,1:T(2,128)(2,1)S(1)} %reshape.535, bf16[16384,384]{1,0:T(8,128)(2,1)} %bitcast.58), kind=kOutput, calls=%fused_computation.8 | convolution fusion | flops 12582912 | bytes 12617216 | tf_op jit(solution)/shard_map/dot_general | solution.py:76
  208.3 96.7 %all-gather.6.cloned.1.call-done = bf16[16384,6,128]{2,0,1:T(8,128)(2,1)} async-done(((bf16[1024,6,128]{2,0,1:T(8,128)(2,1)}), bf16[16384,6,128]{2,0,1:T(8,128)(2,1)}) %all-gather.6.cloned.1.call-update) | async-done | bytes 25165840 | tf_op jit(solution)/shard_map/all_gather | solution.py:69
  305.0 29.9 %copy.34 = bf16[16384,6,128]{0,2,1:T(8,128)(2,1)} copy(bf16[16384,6,128]{2,0,1:T(8,128)(2,1)} %all-gather.6.cloned.1.call-done) | data formatting | bytes 50331648 | tf_op jit(solution)/shard_map/all_gather | solution.py:69
  334.9 18.1 %fusion.14 = f32[384,768]{1,0:T(8,128)} fusion(bf16[16384,384]{1,0:T(8,128)(2,1)} %bitcast.59, bf16[16384,768]{0,1:T(8,128)(2,1)} %bitcast.62), kind=kOutput, calls=%fused_computation.36 | convolution fusion | flops 9663676416 | bytes 38928384 | tf_op jit(solution)/shard_map/dot_general | solution.py:72
  (21 shorter events, 3.7 us)
Async XLA Ops:
  7.2 146.2 %all-gather.4.cloned.1.call-start = ((), (), s32[]{:S(2)}) async-start(), calls=%async_computation.2 | async-start | bytes 14155776 | tf_op jit(solution)/shard_map/all_gather | solution.py:65
  72.2 232.9 %all-gather.6.cloned.1.call-start = ((), (), s32[]{:S(2)}) async-start(), calls=%async_computation.3 | async-start | bytes 26738688 | tf_op jit(solution)/shard_map/all_gather | solution.py:69
  113.3 0.7 copy-start
  113.3 0.7 copy-start.1
Sparse Core Ops, SparseCore 0:
  72.3 81.0 all-gather.3
  155.6 149.4 all-gather.5
where the time goes:
time: 362 us; the launch traced here: 360 us
  waiting for transfers between devices  106 us (29%)
  blocking collectives  98.4 us (27%)
  local copies, waits for them, and re-layouts  80.3 us (22%)
  matrix products  31.7 us (9%)
  other arithmetic  28.8 us (8%)
  between operations  14.8 us (4%)
    all_gather x1, waiting for transfers between devices, on_device(): shard_piece = lax.all_gather(own_cols, 'row', axis=0, tiled=True)  96.7 us
    all_to_all x1, blocking collectives, on_device(): lax.all_to_all(slotted, 'col', split_axis=1, concat_axis=0, tiled=True)  39.8 us
    all_gather x1, local copies, waits for them, and re-layouts, on_device(): shard_piece = lax.all_gather(own_cols, 'row', axis=0, tiled=True)  29.9 us
    all_gather x1, blocking collectives, on_device(): lax.all_gather(white_obs.reshape(local_rows), ('row', 'col'), axis=0, til...  29.7 us
    all_to_all x1, blocking collectives, on_device(): lax.all_to_all(slotted, 'row', split_axis=1, concat_axis=0, tiled=True)  28.9 us
    dot_general x1, matrix products, on_device(): lax.dot_general(row_panel, flat_piece, (((0,), (0,)), ((), ())), preferre...  18.1 us
    transpose x1, local copies, waits for them, and re-layouts, on_device(): jnp.swapaxes(row_panel, 0, 1).reshape(total_rows, row_tiles * tile_size)  17.5 us
    all_gather x1, local copies, waits for them, and re-layouts, on_device(): row_panel = lax.all_gather(own_rows, 'col', axis=0, tiled=True)  16.6 us
  transfers between devices with their start and end apart: 2, of which 2 were waited for; matrix products, arithmetic and copies ran while one was open for 16% of the time, Pallas kernels for 0%

commit v1 on v0

v1 whole, which is shorter than its diff:
```python
import jax
import jax.numpy as jnp
from jax import lax
from jax.experimental import pallas as pl
from jax.experimental.pallas import tpu as pltpu
from jax.sharding import PartitionSpec as P

MESH = pl.DeviceIdType.MESH
F32 = jnp.float32
BF16 = jnp.bfloat16
TB = 128
R_DX = (2, 1, 3, 0)
C_CH = ((0, 2), (2, 2), (4, 2))
NA, NB = len(R_DX), len(C_CH)
N_COPIES = 126


def inverse_factor(lens, amps, decays, gaps, noise, obs):
    shape = (8, TB)
    pos = lax.broadcasted_iota(jnp.int32, shape, 1)
    live = jnp.broadcast_to(gaps, shape).astype(F32)
    noise = jnp.broadcast_to(noise, shape)
    e0 = lens[0, 0]
    e1 = e0 + lens[0, 1]
    e2 = e1 + lens[0, 2]

    def by_arc(p, v):
        return jnp.where(p < e0, v[0], jnp.where(p < e1, v[1], jnp.where(p < e2, v[2], v[3])))

    amp = by_arc(pos, [amps[0, i] for i in range(4)])
    decay = by_arc(pos, [decays[0, i] for i in range(4)])
    start = (pos == 0) | (pos == e0) | (pos == e1) | (pos == e2)
    gain = decay * decay
    q = amp * (1.0 - gain)
    live_prev = pltpu.roll(live, 1, 1) > 0.5
    noise_prev = pltpu.roll(noise, 1, 1)
    a = jnp.where(start, 0.0, jnp.where(live_prev, gain * noise_prev + q, gain))
    b = jnp.where(start, amp, jnp.where(live_prev, q * noise_prev, q))
    c = jnp.where(start, 0.0, jnp.where(live_prev, 1.0, 0.0))
    d = jnp.where(start, 1.0, jnp.where(live_prev, noise_prev, 1.0))
    for shift in (1, 2, 4, 8, 16, 32):
        ok = pos >= shift
        ap, bp = pltpu.roll(a, shift, 1), pltpu.roll(b, shift, 1)
        cp, dp = pltpu.roll(c, shift, 1), pltpu.roll(d, shift, 1)
        an = jnp.where(ok, a * ap + b * cp, a)
        bn = jnp.where(ok, a * bp + b * dp, b)
        cn = jnp.where(ok, c * ap + d * cp, c)
        dn = jnp.where(ok, c * bp + d * dp, d)
        scale = 1.0 / (an + bn + cn + dn)
        a, b, c, d = an * scale, bn * scale, cn * scale, dn * scale
    var = b / d
    is_live = live > 0.5
    total = jnp.where(is_live, var, 0.0) + noise
    root = live * lax.rsqrt(total)
    log_step = jnp.log(jnp.where(is_live, decay * (noise / total), decay))
    push = jnp.where(is_live, decay * (var / total), 0.0)
    sq = (TB, TB)
    row = lax.broadcasted_iota(jnp.int32, sq, 0)
    col = lax.broadcasted_iota(jnp.int32, sq, 1)
    upto = (row <= col).astype(F32)
    cum = jnp.dot(log_step, upto, precision=lax.Precision.HIGHEST, preferred_element_type=F32)
    before = cum - log_step
    eye = row == col

    def as_column(v):
        return jnp.sum(jnp.where(eye, jnp.broadcast_to(v[0:1], sq), 0.0), axis=1, keepdims=True)

    def arc_of(p):
        return by_arc(p, [0, 1, 2, 3])

    inside = (row > col) & (arc_of(row) == arc_of(col))
    span = jnp.where(inside, as_column(before) - cum[0:1], -1e30)
    lower = jnp.where(eye, 1.0, -jnp.exp(span) * push[0:1])
    inv = as_column(root) * lower
    white_col = jnp.sum(inv * obs, axis=1, keepdims=True)
    white_row = jnp.sum(jnp.where(eye, white_col, 0.0), axis=0, keepdims=True)
    return inv, white_row


def kernel(
    tile_map, lens, amps, decays, plan, design, obs, gaps, noise,
    gram, rhs, bal,
    dbuf, wn, wt, pall, rbuf, rsend, cbufs, csends, acc, rss, rsr, obs_all, psend, pbuf, qbuf, tot, tbuf,
    load_sem, ssem, rsem,
):
    r, q = lax.axis_index("row"), lax.axis_index("col")
    x, y, z, c = r // 4, r % 4, q // 2, q % 2

    def dev(dx=0, dy=0, dz=0, dc=0):
        return ((x + dx) % 4 * 4 + (y + dy) % 4, (z + dz) % 4 * 2 + (c + dc) % 2)

    copies = []

    def send(src, dst, to):
        i = len(copies)
        cp = pltpu.make_async_remote_copy(
            src_ref=src, dst_ref=dst, send_sem=ssem.at[i], recv_sem=rsem.at[i], device_id=to, device_id_type=MESH
        )
        cp.start()
        copies.append(cp)
        return cp

    load = pltpu.make_async_copy(design, dbuf, load_sem)
    load.start()
    line = [(dz, dc) for dz in range(4) for dc in range(2) if (dz, dc) != (0, 0)]
    partners = [dev(dx=i) for i in (1, 2, 3)] + [dev(dy=i) for i in (1, 2, 3)] + [dev(dz=i, dc=j) for i, j in line]
    barrier = pltpu.get_barrier_semaphore()
    for p in partners:
        pl.semaphore_signal(barrier, inc=1, device_id=p, device_id_type=MESH)

    inv, white_row = inverse_factor(lens, amps, decays, gaps[...], noise[...], obs[...])
    hi = inv.astype(BF16)
    lo = (inv - hi.astype(F32)).astype(BF16)
    both = jnp.concatenate([hi, lo], axis=1)
    obs_all[r, q] = white_row
    half = jnp.broadcast_to(white_row, (8, TB)).astype(BF16)
    load.wait()

    def whiten_pair(t, carry):
        cols = dbuf[:, pl.ds(pl.multiple_of(t * 256, 256), 256)]
        white = jnp.dot(both, jnp.concatenate([cols, cols], axis=0), preferred_element_type=F32)
        kept = white.astype(BF16)
        flipped = white.T.astype(BF16)
        part = jnp.dot(half, kept, preferred_element_type=F32)
        for i in range(2):
            wn[2 * t + i] = kept[:, i * TB : (i + 1) * TB]
            wt[2 * t + i] = flipped[i * TB : (i + 1) * TB]
            pall[2 * t + i] = part[0:1, i * TB : (i + 1) * TB]
        return carry

    lax.fori_loop(0, 24, whiten_pair, 0, unroll=2)

    for k, dx in enumerate(R_DX):
        for dy in range(4):
            for i in range(3):
                t = tile_map[(x + dx) % 4 * 12 + (y + dy) % 4 * 3 + i]
                rows = pl.ds(i * TB, TB)
                if dy == 0:
                    rbuf[k, 0, 0, 0, rows] = wt[t]
                else:
                    rsend[k, dy - 1, rows] = wt[t]
    for b, (first, count) in enumerate(C_CH):
        for dz in range(4):
            for dc in range(2):
                for i in range(count):
                    t = tile_map[((z + dz) % 4 * 2 + (c + dc) % 2) * 6 + first + i]
                    cols = pl.ds(i * TB, TB)
                    if (dz, dc) == (0, 0):
                        cbufs[b][0, 0, :, cols] = wn[t]
                    else:
                        csends[b][dz * 2 + dc - 1, :, cols] = wn[t]
    for dy in range(4):
        for xx in range(4):
            for i in range(3):
                t = tile_map[xx * 12 + (y + dy) % 4 * 3 + i]
                psend[dy, xx, i : i + 1] = pall[t]

    pl.semaphore_wait(barrier, len(partners))

    partner = dev(dc=1)
    y_up, y_dn, z_up, z_dn = dev(dy=1), dev(dy=3), dev(dz=1), dev(dz=3)

    def spread_r(k):
        return [send(rsend.at[k, d - 1], rbuf.at[k, 0, 0, 4 - d], dev(dy=d)) for d in (1, 3, 2)]

    def spread_c(b):
        return [
            send(csends[b].at[dz * 2 + dc - 1], cbufs[b].at[0, (4 - dz) % 4 * 2 + dc], dev(dz=dz, dc=dc))
            for dz, dc in line
        ]

    def gather1(buf, up, dn, halves):
        first, second = halves
        return [
            send(buf(0, first), buf(3, first), up),
            send(buf(0, second), buf(1, second), dn),
            send(buf(0, second), buf(3, second), up),
            send(buf(0, first), buf(1, first), dn),
        ]

    def gather2(buf, up, dn, halves, sent):
        first, second = halves
        sent[0].wait_recv()
        a = send(buf(3, first), buf(2, first), up)
        sent[1].wait_recv()
        return [a, send(buf(1, second), buf(2, second), dn)]

    r_halves = (pl.ds(0, 2), pl.ds(2, 2))
    c_halves = (pl.ds(0, 4), pl.ds(4, 4))
    r_ref = [lambda rz, part, k=k: rbuf.at[k, rz, 0, part] for k in range(NA)]
    c_ref = [lambda ry, part, b=b: cbufs[b].at[ry, part] for b in range(NB)]
    a2a_r, a2a_c, g1r, g2r, g1c, g2c = {}, {}, {}, {}, {}, {}
    d2d = {k: [] for k in range(NA)}

    def over(k, rz):
        d2d[k].append(send(rbuf.at[k, rz, 0], rbuf.at[k, rz, 1], partner))

    def r1(k):
        for cp in a2a_r[k]:
            cp.wait_recv()
        g1r[k] = gather1(r_ref[k], z_up, z_dn, r_halves)
        over(k, 0)

    def r2(k):
        g2r[k] = gather2(r_ref[k], z_up, z_dn, r_halves, g1r[k])

    def rd(k):
        g1r[k][2].wait_recv()
        over(k, 3)
        g1r[k][3].wait_recv()
        over(k, 1)

    def re(k):
        for cp in g2r[k]:
            cp.wait_recv()
        over(k, 2)

    def rf(k):
        for cp in d2d[k]:
            cp.wait_recv()

    def c1(b):
        for cp in a2a_c[b]:
            cp.wait_recv()
        g1c[b] = gather1(c_ref[b], y_up, y_dn, c_halves)

    def c2(b):
        g2c[b] = gather2(c_ref[b], y_up, y_dn, c_halves, g1c[b])

    def cf(b):
        for cp in g1c[b][2:] + g2c[b]:
            cp.wait_recv()

    reduce = {}

    def block(k, b):
        first, count = C_CH[b]
        out = gram.at[:, pl.ds(first * TB, count * TB)] if R_DX[k] == 0 else acc.at[:, pl.ds(0, count * TB)]

        def product(rz):
            lhs = jnp.concatenate([rbuf[k, rz, rc, ry] for rc in range(2) for ry in range(4)], axis=1)
            right = jnp.concatenate([cbufs[b][ry, rz * 2 + rc] for rc in range(2) for ry in range(4)], axis=0)
            return jnp.dot(lhs, right, preferred_element_type=F32)

        out[...] = product(0)

        def step(rz, carry):
            out[...] += product(rz)
            return carry

        lax.fori_loop(1, 4, step, 0)
        dx = R_DX[k]
        if dx:
            rss[b][dx - 1] = out[...].astype(BF16)
            reduce[b, dx] = send(rss[b].at[dx - 1], rsr[b].at[3 - dx], dev(dx=dx))

    def small1():
        o = [send(obs_all.at[r, q], obs_all.at[r, q], dev(dz=dz, dc=dc)) for dz, dc in line]
        pbuf[y] = psend[0]
        p = [send(psend.at[d], pbuf.at[y], dev(dy=d)) for d in (1, 2, 3)]
        return o + p

    def small2(sent):
        for cp in sent:
            cp.wait_recv()
        o = [send(obs_all.at[r], obs_all.at[r], dev(dy=d)) for d in (1, 2, 3)]
        qbuf[q] = (pbuf[0] + pbuf[1]) + (pbuf[2] + pbuf[3])
        p = [send(qbuf.at[q], qbuf.at[q], dev(dz=dz, dc=dc)) for dz, dc in line]
        return o + p

    def small3(sent):
        for cp in sent:
            cp.wait_recv()
        rows = obs_all.at[pl.ds(4 * x, 4)]
        o = [send(rows, rows, dev(dx=d)) for d in (1, 2, 3)]
        total = qbuf[0]
        for i in range(1, 8):
            total = total + qbuf[i]
        tot[...] = total
        tbuf[x] = tot[x]
        p = [send(tot.at[(x + d) % 4], tbuf.at[x], dev(dx=d)) for d in (1, 2, 3)]
        return o + p

    def small4(sent):
        for cp in sent:
            cp.wait_recv()
        rhs[...] = (tbuf[0] + tbuf[1]) + (tbuf[2] + tbuf[3])
        owner = plan[0]
        bal[...] = obs_all[owner // 8, owner % 8]

    a2a_r[0] = spread_r(0)
    a2a_c[0] = spread_c(0)
    a2a_r[1] = spread_r(1)
    small = small1()
    r1(0)
    c1(0)
    a2a_c[1] = spread_c(1)
    a2a_r[2] = spread_r(2)
    r2(0)
    r1(1)
    c2(0)
    c1(1)
    rd(0)
    a2a_c[2] = spread_c(2)
    a2a_r[3] = spread_r(3)
    re(0)
    rf(0)
    cf(0)
    block(0, 0)
    r2(1)
    r1(2)
    c2(1)
    c1(2)
    rd(1)
    re(1)
    small = small2(small)
    rf(1)
    block(1, 0)
    cf(1)
    block(0, 1)
    block(1, 1)
    r2(2)
    r1(3)
    rd(2)
    c2(2)
    re(2)
    small = small3(small)
    rf(2)
    block(2, 0)
    block(2, 1)
    r2(3)
    rd(3)
    re(3)
    cf(2)
    block(0, 2)
    block(1, 2)
    block(2, 2)
    rf(3)
    for b in range(NB):
        block(3, b)
    small4(small)
    for b, (first, count) in enumerate(C_CH):
        total = gram[:, first * TB : (first + count) * TB]
        for dx in (1, 3, 2):
            reduce[b, dx].wait_recv()
        for i in range(3):
            total = total + rsr[b][i].astype(F32)
        gram[:, first * TB : (first + count) * TB] = total
    for cp in copies:
        cp.wait_send()


def on_device(
    design, observations, gaps, noise_var, arc_lengths, arc_amp, arc_decay, plan, tile_map
):
    smem = pl.BlockSpec(memory_space=pltpu.SMEM)
    vmem = pl.BlockSpec(memory_space=pltpu.VMEM)
    width = [count * TB for _, count in C_CH]
    gram, rhs, bal = pl.pallas_call(
        kernel,
        name="normal_equations",
        out_shape=(
            jax.ShapeDtypeStruct((384, 768), F32),
            jax.ShapeDtypeStruct((3, TB), F32),
            jax.ShapeDtypeStruct((1, TB), F32),
        ),
        in_specs=[smem] * 5 + [pl.BlockSpec(memory_space=pl.ANY)] + [vmem] * 3,
        out_specs=(vmem, vmem, vmem),
        scratch_shapes=[
            pltpu.VMEM((TB, 6144), BF16),
            pltpu.VMEM((48, TB, TB), BF16),
            pltpu.VMEM((48, TB, TB), BF16),
            pltpu.VMEM((48, 1, TB), F32),
            pltpu.VMEM((NA, 4, 2, 4, 384, TB), BF16),
            pltpu.VMEM((NA, 3, 384, TB), BF16),
            [pltpu.VMEM((4, 8, TB, w), BF16) for w in width],
            [pltpu.VMEM((7, TB, w), BF16) for w in width],
            pltpu.VMEM((384, max(width)), F32),
            [pltpu.VMEM((3, 384, w), BF16) for w in width],
            [pltpu.VMEM((3, 384, w), BF16) for w in width],
            pltpu.VMEM((16, 8, 1, TB), F32),
            pltpu.VMEM((4, 4, 3, TB), F32),
            pltpu.VMEM((4, 4, 3, TB), F32),
            pltpu.VMEM((8, 4, 3, TB), F32),
            pltpu.VMEM((4, 3, TB), F32),
            pltpu.VMEM((4, 3, TB), F32),
            pltpu.SemaphoreType.DMA,
            pltpu.SemaphoreType.DMA((N_COPIES,)),
            pltpu.SemaphoreType.DMA((N_COPIES,)),
        ],
        compiler_params=pltpu.CompilerParams(
            collective_id=0, has_side_effects=True, vmem_limit_bytes=60 * 1024 * 1024
        ),
    )(
        tile_map,
        arc_lengths,
        arc_amp,
        arc_decay,
        plan,
        design,
        observations.reshape(1, TB),
        gaps.reshape(1, TB),
        noise_var.reshape(1, TB),
    )
    return gram, rhs.reshape(384), bal


def solution(mesh):
    placed = (
        P(("row", "col"), None),
        P(("row", "col")),
        P(("row", "col")),
        P(("row", "col")),
        P(("row", "col"), None),
        P(("row", "col"), None),
        P(("row", "col"), None),
        P(("row", "col")),
        P(),
    )
    return jax.shard_map(
        on_device,
        mesh=mesh,
        in_specs=placed,
        out_specs=(P("row", "col"), P("row"), P(("row", "col"), None)),
        check_vma=False,
    )
```

time: 362 us -> 110 us (0.30)
  waiting for transfers between devices: 106 us -> 0 us
  Pallas kernels: 0 us -> 105 us
  blocking collectives: 98.4 us -> 0 us
  local copies, waits for them, and re-layouts: 80.3 us -> 3.46 us
  matrix products: 31.7 us -> 0 us
  other arithmetic: 28.8 us -> 0 us
  between operations: 14.8 us -> 1.31 us
    all_gather x2 -> x0, waiting for transfers between devices: 106 us -> none  [the longest x1 96.7 us: on_device(): shard_piece = lax.all_gather(own_cols, 'row', axis=0, tiled=True)]
    pallas_call x0 -> x1, Pallas kernels: none -> 105 us  [on_device(): pl.pallas_call(kernel, name='normal_equations', out_shape=(jax.ShapeDtype...]
    all_to_all x2 -> x0, blocking collectives: 68.7 us -> none  [the longest x1 39.8 us: on_device(): lax.all_to_all(slotted, 'col', split_axis=1, concat_axis=0, tiled=True)]
    all_gather x2 -> x0, local copies, waits for them, and re-layouts: 46.5 us -> none  [the longest x1 29.9 us: on_device(): shard_piece = lax.all_gather(own_cols, 'row', axis=0, tiled=True)]
    all_gather x1 -> x0, blocking collectives: 29.7 us -> none  [on_device(): lax.all_gather(white_obs.reshape(local_rows), ('row', 'col'), axis=0, til...]
    dot_general x2 -> x0, matrix products: 27.2 us -> none  [the longest x1 18.1 us: on_device(): lax.dot_general(row_panel, flat_piece, (((0,), (0,)), ((), ())), preferre...]
    another operation x6 -> x0, other arithmetic: 23.7 us -> none  [the longest x3 12.4 us: whiten(): factor = jnp.linalg.cholesky(covariance)]
    transpose x1 -> x0, local copies, waits for them, and re-layouts: 17.5 us -> none  [on_device(): jnp.swapaxes(row_panel, 0, 1).reshape(total_rows, row_tiles * tile_size)]
  transfers between devices with their start and end apart: 2 -> 0, of which waited for: 2 -> 0; matrix products, arithmetic and copies ran while one was open for 16% -> 0% of each run, Pallas kernels for 0% -> 0%
where the time goes in v1:
time: 110 us; the launch traced here: 109 us
  Pallas kernels  105 us (95%)
  local copies, waits for them, and re-layouts  3.46 us (3%)
  between operations  1.31 us (1%)
    pallas_call x1, Pallas kernels, on_device(): pl.pallas_call(kernel, name='normal_equations', out_shape=(jax.ShapeDtype...  105 us
    unnamed x7, local copies, waits for them, and re-layouts  3.46 us

profile of v1, /device:TPU:1, one launch (start us, length us, event | category | flops | bytes accessed | tf_op | source)
XLA Modules:
  0.0 109.4 jit_solution(12438924193671054937)
XLA Ops:
  1.3 104.6 %normal_equations.1 = (f32[384,768]{1,0:T(8,128)}, f32[3,128]{1,0:T(4,128)}, f32[1,128]{1,0:T(1,128)}) custom-call(s32[48]{0:T(128)} %tile_map.1, s32[1,4]{1,0:T(1,128)} %lens.1, f32[1,4]{1,0:T(1,128)} %amps.1, f32[1,4]{1,0:T(1,128)} %decays.1, s32[1]{0:T(128)S(6)} %copy.15.plan, bf16[128,6144]{1,0:T(8,128)(2,1)} %design.1, f32[1,128]{1,0:T(1,128)} %bitcast.5, ...), custom_call_target="tpu_custom_call" | custom-call | tf_op jit(solution)/shard_map/normal_equations/pallas_call | solution.py:359
  105.9 0.0 copy-start
  105.9 0.0 copy-start.1
  105.9 2.4 %copy.16 = f32[384,768]{1,0:T(8,128)} copy(f32[384,768]{1,0:T(8,128)} %get-tuple-element.12) | data formatting | bytes 2359296
  108.3 0.0 copy-done
  108.3 0.6 copy.17
  108.9 0.0 copy-done.1
  108.9 0.5 copy.18
Async XLA Ops:
  105.9 2.4 %copy-start = (f32[3,128]{1,0:T(4,128)S(1)}, f32[3,128]{1,0:T(4,128)}, u32[]{:S(2)}) copy-start(f32[3,128]{1,0:T(4,128)} %get-tuple-element.7) | copy-start | bytes 4612
  105.9 3.0 %copy-start.1 = (f32[1,128]{1,0:T(1,128)S(1)}, f32[1,128]{1,0:T(1,128)}, u32[]{:S(2)}) copy-start(f32[1,128]{1,0:T(1,128)} %get-tuple-element.14) | copy-start | bytes 1540

commit v2 on v1

v2 whole, which is shorter than its diff:
```python
import jax
import jax.numpy as jnp
from jax import lax
from jax.experimental import pallas as pl
from jax.experimental.pallas import tpu as pltpu
from jax.sharding import PartitionSpec as P

MESH = pl.DeviceIdType.MESH
F32 = jnp.float32
BF16 = jnp.bfloat16
TB = 128
R_CH = (((2, 0, 384),), ((1, 0, 192), (3, 0, 192)), ((1, 192, 192), (3, 192, 192)), ((0, 0, 384),))
C_CH = ((0, 2), (2, 2), (4, 1), (5, 1))
NA, NB, NJ = len(R_CH), len(C_CH), 6
ORDER = (
    (0, 0, 1), (1, 0, 1), (0, 2, 3), (1, 2, 3), (2, 0, 1), (2, 2, 3), (0, 4, 4), (1, 4, 4), (2, 4, 4),
    (0, 5, 5), (1, 5, 5), (2, 5, 5), (3, 0, 1), (3, 2, 3), (3, 4, 5),
)
N_GOT, N_LEFT = 50, 13


def inverse_factor(lens, amps, decays, gaps, noise, obs):
    shape = (8, TB)
    pos = lax.broadcasted_iota(jnp.int32, shape, 1)
    live = jnp.broadcast_to(gaps, shape).astype(F32)
    noise = jnp.broadcast_to(noise, shape)
    e0 = lens[0, 0]
    e1 = e0 + lens[0, 1]
    e2 = e1 + lens[0, 2]

    def by_arc(p, v):
        return jnp.where(p < e0, v[0], jnp.where(p < e1, v[1], jnp.where(p < e2, v[2], v[3])))

    amp = by_arc(pos, [amps[0, i] for i in range(4)])
    decay = by_arc(pos, [decays[0, i] for i in range(4)])
    start = (pos == 0) | (pos == e0) | (pos == e1) | (pos == e2)
    gain = decay * decay
    q = amp * (1.0 - gain)
    live_prev = pltpu.roll(live, 1, 1) > 0.5
    noise_prev = pltpu.roll(noise, 1, 1)
    a = jnp.where(start, 0.0, jnp.where(live_prev, gain * noise_prev + q, gain))
    b = jnp.where(start, amp, jnp.where(live_prev, q * noise_prev, q))
    c = jnp.where(start, 0.0, jnp.where(live_prev, 1.0, 0.0))
    d = jnp.where(start, 1.0, jnp.where(live_prev, noise_prev, 1.0))
    for shift in (1, 2, 4, 8, 16, 32):
        ok = pos >= shift
        ap, bp = pltpu.roll(a, shift, 1), pltpu.roll(b, shift, 1)
        cp, dp = pltpu.roll(c, shift, 1), pltpu.roll(d, shift, 1)
        an = jnp.where(ok, a * ap + b * cp, a)
        bn = jnp.where(ok, a * bp + b * dp, b)
        cn = jnp.where(ok, c * ap + d * cp, c)
        dn = jnp.where(ok, c * bp + d * dp, d)
        scale = 1.0 / (an + bn + cn + dn)
        a, b, c, d = an * scale, bn * scale, cn * scale, dn * scale
    var = b / d
    is_live = live > 0.5
    total = jnp.where(is_live, var, 0.0) + noise
    root = live * lax.rsqrt(total)
    log_step = jnp.log(jnp.where(is_live, decay * (noise / total), decay))
    push = jnp.where(is_live, decay * (var / total), 0.0)
    sq = (TB, TB)
    row = lax.broadcasted_iota(jnp.int32, sq, 0)
    col = lax.broadcasted_iota(jnp.int32, sq, 1)
    upto = (row <= col).astype(F32)
    cum = jnp.dot(log_step, upto, precision=lax.Precision.HIGHEST, preferred_element_type=F32)
    before = cum - log_step
    eye = row == col

    def as_column(v):
        return jnp.sum(jnp.where(eye, jnp.broadcast_to(v[0:1], sq), 0.0), axis=1, keepdims=True)

    def arc_of(p):
        return by_arc(p, [0, 1, 2, 3])

    inside = (row > col) & (arc_of(row) == arc_of(col))
    span = jnp.where(inside, as_column(before) - cum[0:1], -1e30)
    lower = jnp.where(eye, 1.0, -jnp.exp(span) * push[0:1])
    inv = as_column(root) * lower
    white_col = jnp.sum(inv * obs, axis=1, keepdims=True)
    white_row = jnp.sum(jnp.where(eye, white_col, 0.0), axis=0, keepdims=True)
    return inv, white_row


def kernel(
    tile_map, lens, amps, decays, plan, design, obs, gaps, noise,
    gram, rhs, bal,
    vbuf, gbuf, dbuf, wn, wt, pall, rbuf, rsend, cbuf, csend, own, rss, rsr, obs_all, psend, pbuf, qbuf, tot, tbuf,
    load_sem, ssem, rsem, sum_ssem, sum_rsem,
):
    r, q = lax.axis_index("row"), lax.axis_index("col")
    x, y, z, c = r // 4, r % 4, q // 2, q % 2

    def place(dx, dy, dz, dc):
        return ((x + dx) % 4 * 4 + (y + dy) % 4, (z + dz) % 4 * 2 + (c + dc) % 2)

    steps = [(i, 0, 0, 0) for i in (1, 2, 3)] + [(0, i, 0, 0) for i in (1, 2, 3)]
    steps = steps + [(0, 0, i, j) for i in range(4) for j in range(2) if (i, j) != (0, 0)]
    places = {step: place(*step) for step in steps}

    def dev(dx=0, dy=0, dz=0, dc=0):
        return places[dx, dy, dz, dc]

    x_of = [(x + d) % 4 for d in range(4)]
    x_rows = pl.ds(4 * x, 4)

    got, left = {}, {}

    def group(table, sems, name, region):
        if name not in table:
            table[name] = (len(table), sems, region)
        return table[name][0]

    def wait(table, name):
        i, sems, region = table[name]
        pltpu.make_async_copy(region(), region(), sems.at[i]).wait()

    def send(src, dst, to, arrival, leaving):
        pltpu.make_async_remote_copy(
            src_ref=src, dst_ref=dst, send_sem=ssem.at[group(left, ssem, *leaving)], recv_sem=rsem.at[group(got, rsem, *arrival)],
            device_id=to, device_id_type=MESH,
        ).start()

    load = pltpu.make_async_copy(design, dbuf, load_sem.at[0])
    vectors = [
        pltpu.make_async_copy(ref, vbuf.at[i], load_sem.at[1 + i]) for i, ref in enumerate((obs, noise))
    ] + [pltpu.make_async_copy(gaps, gbuf, load_sem.at[3])]
    line = [(dz, dc) for dz in range(4) for dc in range(2) if (dz, dc) != (0, 0)]
    barrier = pltpu.get_barrier_semaphore()
    for p in places.values():
        pl.semaphore_signal(barrier, inc=1, device_id=p, device_id_type=MESH)

    for cp in vectors:
        cp.start()
    load.start()
    for cp in vectors:
        cp.wait()
    inv, white_row = inverse_factor(lens, amps, decays, gbuf[...], vbuf[1], vbuf[0])
    hi = inv.astype(BF16)
    lo = (inv - hi.astype(F32)).astype(BF16)
    both = jnp.concatenate([hi, lo], axis=1)
    obs_all[r, q] = white_row
    half = jnp.broadcast_to(white_row, (8, TB)).astype(BF16)
    load.wait()

    def whiten_pair(t, carry):
        cols = dbuf[:, pl.ds(pl.multiple_of(t * 256, 256), 256)]
        white = jnp.dot(both, jnp.concatenate([cols, cols], axis=0), preferred_element_type=F32)
        kept = white.astype(BF16)
        flipped = white.T.astype(BF16)
        for i in range(2):
            wn[2 * t + i] = kept[:, i * TB : (i + 1) * TB]
            wt[2 * t + i] = flipped[i * TB : (i + 1) * TB]
        return carry

    lax.fori_loop(0, 24, whiten_pair, 0, unroll=6)

    def stage_r(k):
        for dy in range(4):
            at = 0
            for dx, first, count in R_CH[k]:
                for i in range(3):
                    lo, hi = max(first, i * TB), min(first + count, i * TB + TB)
                    if lo < hi:
                        t = tile_map[(x + dx) % 4 * 12 + (y + dy) % 4 * 3 + i]
                        tile = wt[t, pl.ds(lo - i * TB, hi - lo)]
                        if dy == 0:
                            rbuf[k, 0, 0, 0, pl.ds(at, hi - lo)] = tile
                        else:
                            rsend[k, dy - 1, pl.ds(at, hi - lo)] = tile
                        at += hi - lo

    def stage_c(b):
        first, count = C_CH[b]
        for dz in range(4):
            for dc in range(2):
                for j in range(first, first + count):
                    t = tile_map[((z + dz) % 4 * 2 + (c + dc) % 2) * 6 + j]
                    if (dz, dc) == (0, 0):
                        cbuf[j, 0, 0] = wn[t]
                    else:
                        csend[j, dz * 2 + dc - 1] = wn[t]

    stage_r(0)
    stage_c(0)
    stage_r(1)
    stage_c(1)
    pl.semaphore_wait(barrier, len(places))

    partner = dev(dc=1)
    y_up, y_dn, z_up, z_dn = dev(dy=1), dev(dy=3), dev(dz=1), dev(dz=3)

    r_left, c_left = ("r", lambda: rsend), ("c", lambda: csend)
    r1_left, r2_left = ("r1", lambda: rbuf.at[0]), ("r2", lambda: rbuf.at[0, pl.ds(0, 2)])
    c1_left, c2_left = ("c1", lambda: cbuf.at[pl.ds(0, 3)]), ("c2", lambda: cbuf.at[pl.ds(0, 3), pl.ds(0, 2)])
    over_left = ("over", lambda: rbuf.at[pl.ds(0, 2)])

    def tiles(b):
        return pl.ds(*C_CH[b])

    def spread_r(k):
        arrival = (f"r{k}", lambda: rbuf.at[k, 0, 0, pl.ds(1, 3)])
        for d in (1, 3, 2):
            send(rsend.at[k, d - 1], rbuf.at[k, 0, 0, 4 - d], dev(dy=d), arrival, r_left)

    def spread_c(b):
        arrival = (f"c{b}", lambda: cbuf.at[tiles(b), 0, pl.ds(1, 7)])
        for dz, dc in line:
            src = csend.at[tiles(b), dz * 2 + dc - 1]
            send(src, cbuf.at[tiles(b), 0, (4 - dz) % 4 * 2 + dc], dev(dz=dz, dc=dc), arrival, c_left)

    def r_ref(k, rz, part):
        return rbuf.at[k, rz, 0, part]

    def c_ref(b, ry, part):
        return cbuf.at[tiles(b), ry, part]

    def gather1(ref, i, up, dn, halves, name, leaving):
        first, second = halves
        wait(got, f"{name}{i}")
        one, other = (f"{name}up{i}", lambda: ref(i, 3, first)), (f"{name}dn{i}", lambda: ref(i, 1, second))
        rest = (f"{name}rest{i}", lambda: ref(i, 1, pl.ds(0, 2 * first.size)))
        send(ref(i, 0, first), ref(i, 3, first), up, one, leaving)
        send(ref(i, 0, second), ref(i, 1, second), dn, other, leaving)
        send(ref(i, 0, second), ref(i, 3, second), up, rest, leaving)
        send(ref(i, 0, first), ref(i, 1, first), dn, rest, leaving)

    def gather2(ref, i, up, dn, halves, name, leaving):
        first, second = halves
        far = (f"{name}far{i}", lambda: ref(i, 2, pl.ds(0, 2 * first.size)))
        wait(got, f"{name}up{i}")
        send(ref(i, 3, first), ref(i, 2, first), up, far, leaving)
        wait(got, f"{name}dn{i}")
        send(ref(i, 1, second), ref(i, 2, second), dn, far, leaving)

    r_halves = (pl.ds(0, 2), pl.ds(2, 2))
    c_halves = (pl.ds(0, 4), pl.ds(4, 4))

    def over(k, rz):
        send(rbuf.at[k, rz, 0], rbuf.at[k, rz, 1], partner, (f"over{k}", lambda: rbuf.at[k, :, 1]), over_left)

    def r1(k):
        gather1(r_ref, k, z_up, z_dn, r_halves, "r", r1_left)
        over(k, 0)

    def r2(k):
        gather2(r_ref, k, z_up, z_dn, r_halves, "r", r2_left)

    def rd(k):
        wait(got, f"rrest{k}")
        over(k, 3)
        over(k, 1)

    def re(k):
        wait(got, f"rfar{k}")
        over(k, 2)

    def rf(k):
        wait(got, f"over{k}")

    def c1(b):
        gather1(c_ref, b, y_up, y_dn, c_halves, "c", c1_left)

    def c2(b):
        gather2(c_ref, b, y_up, y_dn, c_halves, "c", c2_left)

    def cf(b):
        wait(got, f"crest{b}")
        wait(got, f"cfar{b}")

    def pick(s, values):
        out = values[0]
        for i in range(1, len(values)):
            out = jnp.where(s == i, values[i], out)
        return out

    def block(s):
        k, j, j2 = (pick(s, [block[i] for block in ORDER]) for i in range(3))
        groups = [(rz, rc, ry) for rz in range(4) for rc in range(2) for ry in range(4)]
        lhs = jnp.concatenate([rbuf[k, rz, rc, ry] for rz, rc, ry in groups], axis=1)
        left = jnp.concatenate([cbuf[j, ry, rz * 2 + rc] for rz, rc, ry in groups], axis=0)
        right = jnp.concatenate([cbuf[j2, ry, rz * 2 + rc] for rz, rc, ry in groups], axis=0)
        value = jnp.dot(lhs, jnp.concatenate([left, right], axis=1), preferred_element_type=F32)
        last = k == NA - 1
        own[jnp.where(last, j, NJ)] = value[:, :TB]
        own[jnp.where(last, j2, NJ)] = value[:, TB:]
        rss[j, k] = value[:, :TB].astype(BF16)
        rss[j2, k] = value[:, TB:].astype(BF16)

        @pl.when(k == 0)
        def _():
            to = place(2, 0, 0, 0)
            reduce(j, k, 0, to).start()

            @pl.when(j2 > j)
            def _():
                reduce(j2, k, 0, to).start()

        @pl.when((k == 1) | (k == 2))
        def _():
            up, dn = place(1, 0, 0, 0), place(3, 0, 0, 0)
            reduce(j, k, 1, up).start()
            reduce(j, k, 3, dn).start()

            @pl.when(j2 > j)
            def _():
                reduce(j2, k, 1, up).start()
                reduce(j2, k, 3, dn).start()

    def reduce(j, k, dx, to):
        if dx == 0:
            src, dst = rss.at[j, k], rsr.at[j, 2]
        else:
            src = rss.at[j, k, pl.ds(192 * (dx // 2), 192)]
            dst = rsr.at[j, 4 - dx, pl.ds((k - 1) * 192, 192)]
        return pltpu.make_async_remote_copy(
            src_ref=src, dst_ref=dst, send_sem=sum_ssem, recv_sem=sum_rsem.at[j],
            device_id=to, device_id_type=MESH,
        )

    def small1():
        def partial(t, carry):
            part = jnp.dot(half, jnp.concatenate([wn[2 * t], wn[2 * t + 1]], axis=1), preferred_element_type=F32)
            for i in range(2):
                pall[2 * t + i] = part[0:1, i * TB : (i + 1) * TB]
            return carry

        lax.fori_loop(0, 24, partial, 0, unroll=6)
        for dy in range(4):
            for xx in range(4):
                for i in range(3):
                    t = tile_map[xx * 12 + (y + dy) % 4 * 3 + i]
                    psend[dy, xx, i : i + 1] = pall[t]
        o_in, o_out = (("o1", lambda: obs_all.at[r, pl.ds(0, 7)]),) * 2
        for dz, dc in line:
            send(obs_all.at[r, q], obs_all.at[r, q], dev(dz=dz, dc=dc), o_in, o_out)
        pbuf[y] = psend[0]
        p_in, p_out = ("p1", lambda: pbuf.at[pl.ds(0, 3)]), ("p1", lambda: psend.at[pl.ds(1, 3)])
        for d in (1, 2, 3):
            send(psend.at[d], pbuf.at[y], dev(dy=d), p_in, p_out)

    def small2():
        wait(got, "o1")
        wait(got, "p1")
        o_in, o_out = (("o2", lambda: obs_all.at[pl.ds(0, 3)]),) * 2
        for d in (1, 2, 3):
            send(obs_all.at[r], obs_all.at[r], dev(dy=d), o_in, o_out)
        qbuf[q] = (pbuf[0] + pbuf[1]) + (pbuf[2] + pbuf[3])
        p_in, p_out = (("p2", lambda: qbuf.at[pl.ds(0, 7)]),) * 2
        for dz, dc in line:
            send(qbuf.at[q], qbuf.at[q], dev(dz=dz, dc=dc), p_in, p_out)

    def small3():
        wait(got, "o2")
        wait(got, "p2")
        o_in, o_out = (("o3", lambda: obs_all.at[pl.ds(0, 12)]),) * 2
        for d in (1, 2, 3):
            send(obs_all.at[x_rows], obs_all.at[x_rows], dev(dx=d), o_in, o_out)
        total = qbuf[0]
        for i in range(1, 8):
            total = total + qbuf[i]
        tot[...] = total
        tbuf[x] = tot[x]
        p_in, p_out = ("p3", lambda: tbuf.at[pl.ds(0, 3)]), ("p3", lambda: tot.at[pl.ds(0, 3)])
        for d in (1, 2, 3):
            send(tot.at[x_of[d]], tbuf.at[x], dev(dx=d), p_in, p_out)

    def small4():
        wait(got, "o3")
        wait(got, "p3")
        rhs[...] = (tbuf[0] + tbuf[1]) + (tbuf[2] + tbuf[3])
        every = obs_all[...].reshape(16 * 8, 1, TB)
        block_of = lax.broadcasted_iota(jnp.int32, every.shape, 0)
        bal[...] = jnp.sum(jnp.where(block_of == plan[...], every, 0.0), axis=0)

    spread_r(0)
    spread_c(0)
    spread_r(1)
    spread_c(1)
    stage_r(2)
    stage_c(2)
    stage_r(3)
    stage_c(3)
    r1(0)
    c1(0)
    small1()
    r2(0)
    r1(1)
    c2(0)
    spread_r(2)
    spread_c(2)
    c1(1)
    rd(0)
    re(0)
    spread_r(3)
    spread_c(3)
    r2(1)
    r1(2)
    small2()
    rf(0)
    cf(0)
    c2(1)
    c1(2)

    def before1():
        rd(1)
        re(1)
        r2(2)
        r1(3)
        rf(1)

    def before2():
        c2(2)
        c1(3)
        cf(1)

    def before4():
        rd(2)
        re(2)
        r2(3)
        rf(2)

    def before6():
        cf(2)
        c2(3)

    def before8():
        rd(3)

    def before9():
        small3()
        re(3)
        cf(3)

    def before12():
        rf(3)

    acts = (
        (1, before1), (2, before2), (4, before4), (6, before6), (8, before8), (9, before9), (12, before12),
    )

    def slot(s, carry):
        for i, act in acts:
            pl.when(s == i)(act)
        block(s)
        return carry

    lax.fori_loop(0, len(ORDER), slot, 0)
    small4()
    for j in range(NJ):
        arrived = rsr.at[j, pl.ds(1, 3)]
        pltpu.make_async_copy(arrived, arrived, sum_rsem.at[j]).wait()
        total = own[j]
        for dx in (1, 2, 3):
            total = total + rsr[j, dx].astype(F32)
        gram[:, j * TB : (j + 1) * TB] = total
    for name in left:
        wait(left, name)
    sent = rss.at[:, pl.ds(0, 3)]
    pltpu.make_async_copy(sent, sent, sum_ssem).wait()


def on_device(
    design, observations, gaps, noise_var, arc_lengths, arc_amp, arc_decay, plan, tile_map
):
    smem = pl.BlockSpec(memory_space=pltpu.SMEM)
    vmem = pl.BlockSpec(memory_space=pltpu.VMEM)
    gram, rhs, bal = pl.pallas_call(
        kernel,
        name="normal_equations",
        out_shape=(
            pltpu.VMEM((384, 768), F32),
            pltpu.VMEM((3, TB), F32),
            pltpu.VMEM((1, TB), F32),
        ),
        in_specs=[smem] * 4 + [vmem] + [pl.BlockSpec(memory_space=pl.ANY)] * 4,
        out_specs=(vmem, vmem, vmem),
        scratch_shapes=[
            pltpu.VMEM((2, 1, TB), F32),
            pltpu.VMEM((1, TB), jnp.int32),
            pltpu.VMEM((TB, 6144), BF16),
            pltpu.VMEM((48, TB, TB), BF16),
            pltpu.VMEM((48, TB, TB), BF16),
            pltpu.VMEM((48, 1, TB), F32),
            pltpu.VMEM((NA, 4, 2, 4, 384, TB), BF16),
            pltpu.VMEM((NA, 3, 384, TB), BF16),
            pltpu.VMEM((NJ, 4, 8, TB, TB), BF16),
            pltpu.VMEM((NJ, 7, TB, TB), BF16),
            pltpu.VMEM((NJ + 1, 384, TB), F32),
            pltpu.VMEM((NJ, 4, 384, TB), BF16),
            pltpu.VMEM((NJ, 4, 384, TB), BF16),
            pltpu.VMEM((16, 8, 1, TB), F32),
            pltpu.VMEM((4, 4, 3, TB), F32),
            pltpu.VMEM((4, 4, 3, TB), F32),
            pltpu.VMEM((8, 4, 3, TB), F32),
            pltpu.VMEM((4, 3, TB), F32),
            pltpu.VMEM((4, 3, TB), F32),
            pltpu.SemaphoreType.DMA((4,)),
            pltpu.SemaphoreType.DMA((N_LEFT,)),
            pltpu.SemaphoreType.DMA((N_GOT,)),
            pltpu.SemaphoreType.DMA,
            pltpu.SemaphoreType.DMA((NJ,)),
        ],
        compiler_params=pltpu.CompilerParams(
            collective_id=0, has_side_effects=True, vmem_limit_bytes=60 * 1024 * 1024
        ),
    )(
        tile_map,
        arc_lengths,
        arc_amp,
        arc_decay,
        plan.reshape(1, 1),
        design,
        observations.reshape(1, TB),
        gaps.reshape(1, TB),
        noise_var.reshape(1, TB),
    )
    return gram, rhs.reshape(384), bal


def solution(mesh):
    placed = (
        P(("row", "col"), None),
        P(("row", "col")),
        P(("row", "col")),
        P(("row", "col")),
        P(("row", "col"), None),
        P(("row", "col"), None),
        P(("row", "col"), None),
        P(("row", "col")),
        P(),
    )
    return jax.shard_map(
        on_device,
        mesh=mesh,
        in_specs=placed,
        out_specs=(P("row", "col"), P("row"), P(("row", "col"), None)),
        check_vma=False,
    )
```

time: 110 us -> 93.8 us (0.85)
  Pallas kernels: 105 us -> 90.3 us
  local copies, waits for them, and re-layouts: 3.46 us -> 2.1 us
    pallas_call x1, Pallas kernels: 105 us -> 90.3 us  [on_device(): pl.pallas_call(kernel, name='normal_equations', out_shape=(pltpu.VMEM((38...]
    unnamed x7 -> x3, local copies, waits for them, and re-layouts: 3.46 us -> 2.1 us
where the time goes in v2:
time: 93.8 us; the launch traced here: 93.7 us
  Pallas kernels  90.3 us (96%)
  local copies, waits for them, and re-layouts  2.1 us (2%)
  between operations  1.29 us (1%)
    pallas_call x1, Pallas kernels, on_device(): pl.pallas_call(kernel, name='normal_equations', out_shape=(pltpu.VMEM((38...  90.3 us
    unnamed x3, local copies, waits for them, and re-layouts  2.1 us

profile of v2, /device:TPU:1, one launch (start us, length us, event | category | flops | bytes accessed | tf_op | source)
XLA Modules:
  0.0 93.7 jit_solution(11437371430308049222)
XLA Ops:
  1.3 90.3 %normal_equations.1 = (f32[384,768]{1,0:T(8,128)S(1)}, f32[3,128]{1,0:T(4,128)S(1)}, f32[1,128]{1,0:T(1,128)S(1)}) custom-call(s32[48]{0:T(128)} %tile_map.1, s32[1,4]{1,0:T(1,128)} %lens.1, f32[1,4]{1,0:T(1,128)} %amps.1, f32[1,4]{1,0:T(1,128)} %decays.1, s32[1,1]{1,0:T(1,128)} %bitcast.5.plan, bf16[128,6144]{1,0:T(8,128)(2,1)} %design.1, ...), custom_call_target="tpu_custom_call" | custom-call | tf_op jit(solution)/shard_map/normal_equations/pallas_call | solution.py:467
  91.6 1.0 %copy.15 = f32[384,768]{1,0:T(8,128)} copy(f32[384,768]{1,0:T(8,128)S(1)} %get-tuple-element.9) | data formatting | bytes 2359296
  92.6 0.6 copy.16
  93.2 0.5 copy.17

commit v3 on v2

--- a/solution.py
+++ b/solution.py
@@ -84,7 +84,7 @@
 def kernel(
     tile_map, lens, amps, decays, plan, design, obs, gaps, noise,
     gram, rhs, bal,
-    vbuf, gbuf, dbuf, wn, wt, pall, rbuf, rsend, cbuf, csend, own, rss, rsr, obs_all, psend, pbuf, qbuf, tot, tbuf,
+    dbuf, wn, wt, pall, rbuf, rsend, cbuf, csend, own, rss, rsr, obs_all, psend, pbuf, qbuf, tot, tbuf,
     load_sem, ssem, rsem, sum_ssem, sum_rsem,
 ):
     r, q = lax.axis_index("row"), lax.axis_index("col")
@@ -120,31 +120,30 @@
             device_id=to, device_id_type=MESH,
         ).start()
 
-    load = pltpu.make_async_copy(design, dbuf, load_sem.at[0])
-    vectors = [
-        pltpu.make_async_copy(ref, vbuf.at[i], load_sem.at[1 + i]) for i, ref in enumerate((obs, noise))
-    ] + [pltpu.make_async_copy(gaps, gbuf, load_sem.at[3])]
+    for t in range(48):
+        pltpu.make_async_copy(design.at[:, pl.ds(t * TB, TB)], dbuf.at[t], load_sem).start()
     line = [(dz, dc) for dz in range(4) for dc in range(2) if (dz, dc) != (0, 0)]
     barrier = pltpu.get_barrier_semaphore()
     for p in places.values():
         pl.semaphore_signal(barrier, inc=1, device_id=p, device_id_type=MESH)
 
-    for cp in vectors:
-        cp.start()
-    load.start()
-    for cp in vectors:
-        cp.wait()
-    inv, white_row = inverse_factor(lens, amps, decays, gbuf[...], vbuf[1], vbuf[0])
+    inv, white_row = inverse_factor(lens, amps, decays, gaps[...], noise[...], obs[...])
     hi = inv.astype(BF16)
     lo = (inv - hi.astype(F32)).astype(BF16)
     both = jnp.concatenate([hi, lo], axis=1)
     obs_all[r, q] = white_row
     half = jnp.broadcast_to(white_row, (8, TB)).astype(BF16)
-    load.wait()
+    pltpu.make_async_copy(dbuf, dbuf, load_sem).wait()
+
+    def whitened(cols):
+        return jnp.dot(both, jnp.concatenate([cols, cols], axis=0), preferred_element_type=F32)
+
+    def slot_pair(s, s2):
+        cols = [dbuf[tile_map[i]] for i in (s, s2)]
+        return whitened(jnp.concatenate(cols, axis=1))
 
     def whiten_pair(t, carry):
-        cols = dbuf[:, pl.ds(pl.multiple_of(t * 256, 256), 256)]
-        white = jnp.dot(both, jnp.concatenate([cols, cols], axis=0), preferred_element_type=F32)
+        white = whitened(jnp.concatenate([dbuf[2 * t], dbuf[2 * t + 1]], axis=1))
         kept = white.astype(BF16)
         flipped = white.T.astype(BF16)
         for i in range(2):
@@ -152,7 +151,6 @@
             wt[2 * t + i] = flipped[i * TB : (i + 1) * TB]
         return carry
 
-    lax.fori_loop(0, 24, whiten_pair, 0, unroll=6)
 
     def stage_r(k):
         for dy in range(4):
@@ -180,12 +178,6 @@
                     else:
                         csend[j, dz * 2 + dc - 1] = wn[t]
 
-    stage_r(0)
-    stage_c(0)
-    stage_r(1)
-    stage_c(1)
-    pl.semaphore_wait(barrier, len(places))
-
     partner = dev(dc=1)
     y_up, y_dn, z_up, z_dn = dev(dy=1), dev(dy=3), dev(dz=1), dev(dz=3)
 
@@ -214,13 +206,17 @@
     def c_ref(b, ry, part):
         return cbuf.at[tiles(b), ry, part]
 
+    def pieces(part):
+        return [pl.ds(i, 1) for i in range(part.start, part.start + part.size)]
+
     def gather1(ref, i, up, dn, halves, name, leaving):
         first, second = halves
         wait(got, f"{name}{i}")
         one, other = (f"{name}up{i}", lambda: ref(i, 3, first)), (f"{name}dn{i}", lambda: ref(i, 1, second))
         rest = (f"{name}rest{i}", lambda: ref(i, 1, pl.ds(0, 2 * first.size)))
-        send(ref(i, 0, first), ref(i, 3, first), up, one, leaving)
-        send(ref(i, 0, second), ref(i, 1, second), dn, other, leaving)
+        for p, p2 in zip(pieces(first), pieces(second)):
+            send(ref(i, 0, p), ref(i, 3, p), up, one, leaving)
+            send(ref(i, 0, p2), ref(i, 1, p2), dn, other, leaving)
         send(ref(i, 0, second), ref(i, 3, second), up, rest, leaving)
         send(ref(i, 0, first), ref(i, 1, first), dn, rest, leaving)
 
@@ -228,9 +224,11 @@
         first, second = halves
         far = (f"{name}far{i}", lambda: ref(i, 2, pl.ds(0, 2 * first.size)))
         wait(got, f"{name}up{i}")
-        send(ref(i, 3, first), ref(i, 2, first), up, far, leaving)
+        for p in pieces(first):
+            send(ref(i, 3, p), ref(i, 2, p), up, far, leaving)
         wait(got, f"{name}dn{i}")
-        send(ref(i, 1, second), ref(i, 2, second), dn, far, leaving)
+        for p in pieces(second):
+            send(ref(i, 1, p), ref(i, 2, p), dn, far, leaving)
 
     r_halves = (pl.ds(0, 2), pl.ds(2, 2))
     c_halves = (pl.ds(0, 4), pl.ds(4, 4))
@@ -372,8 +370,32 @@
         block_of = lax.broadcasted_iota(jnp.int32, every.shape, 0)
         bal[...] = jnp.sum(jnp.where(block_of == plan[...], every, 0.0), axis=0)
 
+    first_r = [(dy, i) for dy in (1, 2, 3, 0) for i in range(3)]
+    for n in range(0, 12, 2):
+        pair = first_r[n : n + 2]
+        white = slot_pair(*[(x + R_CH[0][0][0]) % 4 * 12 + (y + dy) % 4 * 3 + i for dy, i in pair])
+        flipped = white.T.astype(BF16)
+        for m, (dy, i) in enumerate(pair):
+            tile, rows = flipped[m * TB : (m + 1) * TB], pl.ds(i * TB, TB)
+            if dy == 0:
+                rbuf[0, 0, 0, 0, rows] = tile
+            else:
+                rsend[0, dy - 1, rows] = tile
+    pl.semaphore_wait(barrier, len(places))
     spread_r(0)
+    for dz, dc in line + [(0, 0)]:
+        base = ((z + dz) % 4 * 2 + (c + dc) % 2) * 6
+        white = slot_pair(base, base + 1).astype(BF16)
+        for j in range(2):
+            tile = white[:, j * TB : (j + 1) * TB]
+            if (dz, dc) == (0, 0):
+                cbuf[j, 0, 0] = tile
+            else:
+                csend[j, dz * 2 + dc - 1] = tile
     spread_c(0)
+    lax.fori_loop(0, 24, whiten_pair, 0, unroll=6)
+    stage_r(1)
+    stage_c(1)
     spread_r(1)
     spread_c(1)
     stage_r(2)
@@ -391,39 +413,39 @@
     c1(1)
     rd(0)
     re(0)
-    spread_r(3)
-    spread_c(3)
     r2(1)
     r1(2)
+    spread_c(3)
+    spread_r(3)
     small2()
     rf(0)
     cf(0)
     c2(1)
-    c1(2)
 
     def before1():
         rd(1)
         re(1)
+        c1(2)
         r2(2)
         r1(3)
         rf(1)
 
     def before2():
+        cf(1)
+
+    def before4():
         c2(2)
         c1(3)
-        cf(1)
-
-    def before4():
         rd(2)
         re(2)
+        rf(2)
+
+    def before6():
         r2(3)
-        rf(2)
-
-    def before6():
         cf(2)
+
+    def before8():
         c2(3)
-
-    def before8():
         rd(3)
 
     def before9():
@@ -459,6 +481,17 @@
     pltpu.make_async_copy(sent, sent, sum_ssem).wait()
 
 
+def hand_over(gram, rhs, bal, gram_out, rhs_out, bal_out, flat, sem):
+    for i in range(3):
+        flat[i * TB : (i + 1) * TB] = rhs[i]
+    pairs = ((gram, gram_out), (bal, bal_out), (flat, rhs_out))
+    copies = [pltpu.make_async_copy(src, dst, sem.at[i]) for i, (src, dst) in enumerate(pairs)]
+    for cp in copies:
+        cp.start()
+    for cp in copies:
+        cp.wait()
+
+
 def on_device(
     design, observations, gaps, noise_var, arc_lengths, arc_amp, arc_decay, plan, tile_map
 ):
@@ -472,12 +505,10 @@
             pltpu.VMEM((3, TB), F32),
             pltpu.VMEM((1, TB), F32),
         ),
-        in_specs=[smem] * 4 + [vmem] + [pl.BlockSpec(memory_space=pl.ANY)] * 4,
+        in_specs=[smem] * 4 + [vmem, pl.BlockSpec(memory_space=pl.ANY)] + [vmem] * 3,
         out_specs=(vmem, vmem, vmem),
         scratch_shapes=[
-            pltpu.VMEM((2, 1, TB), F32),
-            pltpu.VMEM((1, TB), jnp.int32),
-            pltpu.VMEM((TB, 6144), BF16),
+            pltpu.VMEM((48, TB, TB), BF16),
             pltpu.VMEM((48, TB, TB), BF16),
             pltpu.VMEM((48, TB, TB), BF16),
             pltpu.VMEM((48, 1, TB), F32),
@@ -494,7 +525,7 @@
             pltpu.VMEM((8, 4, 3, TB), F32),
             pltpu.VMEM((4, 3, TB), F32),
             pltpu.VMEM((4, 3, TB), F32),
-            pltpu.SemaphoreType.DMA((4,)),
+            pltpu.SemaphoreType.DMA,
             pltpu.SemaphoreType.DMA((N_LEFT,)),
             pltpu.SemaphoreType.DMA((N_GOT,)),
             pltpu.SemaphoreType.DMA,
@@ -514,7 +545,21 @@
         gaps.reshape(1, TB),
         noise_var.reshape(1, TB),
     )
-    return gram, rhs.reshape(384), bal
+    inner = [pltpu.with_memory_space_constraint(v, pltpu.VMEM) for v in (gram, rhs, bal)]
+    anywhere = pl.BlockSpec(memory_space=pl.ANY)
+    return pl.pallas_call(
+        hand_over,
+        name="hand_over",
+        out_shape=(
+            jax.ShapeDtypeStruct((384, 768), F32),
+            jax.ShapeDtypeStruct((384,), F32),
+            jax.ShapeDtypeStruct((1, TB), F32),
+        ),
+        in_specs=[vmem] * 3,
+        out_specs=(anywhere, anywhere, anywhere),
+        scratch_shapes=[pltpu.VMEM((384,), F32), pltpu.SemaphoreType.DMA((3,))],
+        compiler_params=pltpu.CompilerParams(vmem_limit_bytes=1024 * 1024),
+    )(*inner)
 
 
 def solution(mesh):

time: 93.8 us -> 89.8 us (0.957)
  local copies, waits for them, and re-layouts: 2.1 us -> 0 us
  Pallas kernels: 90.3 us -> 88.2 us
    pallas_call x1, Pallas kernels: 90.3 us -> 87.2 us  [on_device(): pl.pallas_call(kernel, name='normal_equations', out_shape=(pltpu.VMEM((38...]
    unnamed x3 -> x0, local copies, waits for them, and re-layouts: 2.1 us -> none
    pallas_call x0 -> x1, Pallas kernels: none -> 1.05 us  [on_device(): pl.pallas_call(hand_over, name='hand_over', out_shape=(jax.ShapeDtypeStru...]
where the time goes in v3:
time: 89.8 us; the launch traced here: 89.5 us
  Pallas kernels  88.2 us (98%)
  between operations  1.29 us (1%)
    pallas_call x1, Pallas kernels, on_device(): pl.pallas_call(kernel, name='normal_equations', out_shape=(pltpu.VMEM((38...  87.2 us

profile of v3, /device:TPU:1, one launch (start us, length us, event | category | flops | bytes accessed | tf_op | source)
XLA Modules:
  0.0 89.5 jit_solution(14404641184551506150)
XLA Ops:
  1.3 87.2 %normal_equations.1 = (f32[384,768]{1,0:T(8,128)S(1)}, f32[3,128]{1,0:T(4,128)S(1)}, f32[1,128]{1,0:T(1,128)S(1)}) custom-call(s32[48]{0:T(128)} %tile_map.1, s32[1,4]{1,0:T(1,128)} %lens.1, f32[1,4]{1,0:T(1,128)} %amps.1, f32[1,4]{1,0:T(1,128)} %decays.1, s32[1,1]{1,0:T(1,128)} %bitcast.4.plan, bf16[128,6144]{1,0:T(8,128)(2,1)} %design.1, ...), custom_call_target="tpu_custom_call" | custom-call | tf_op jit(solution)/shard_map/normal_equations/pallas_call | solution.py:500
  88.5 1.0 %hand_over.1 = (f32[384,768]{1,0:T(8,128)}, f32[384]{0:T(512)}, f32[1,128]{1,0:T(1,128)}) custom-call(f32[384,768]{1,0:T(8,128)S(1)} %get-tuple-element.6.gram, f32[3,128]{1,0:T(4,128)S(1)} %get-tuple-element.7.rhs, f32[1,128]{1,0:T(1,128)S(1)} %get-tuple-element.8.bal), custom_call_target="tpu_custom_call" | custom-call | tf_op jit(solution)/shard_map/hand_over/pallas_call | solution.py:550

commit v4 on v3

--- a/solution.py
+++ b/solution.py
@@ -50,8 +50,10 @@
         bn = jnp.where(ok, a * bp + b * dp, b)
         cn = jnp.where(ok, c * ap + d * cp, c)
         dn = jnp.where(ok, c * bp + d * dp, d)
-        scale = 1.0 / (an + bn + cn + dn)
-        a, b, c, d = an * scale, bn * scale, cn * scale, dn * scale
+        if shift == 8:
+            scale = 1.0 / (an + bn + cn + dn)
+            an, bn, cn, dn = an * scale, bn * scale, cn * scale, dn * scale
+        a, b, c, d = an, bn, cn, dn
     var = b / d
     is_live = live > 0.5
     total = jnp.where(is_live, var, 0.0) + noise
@@ -342,10 +344,11 @@
         o_in, o_out = (("o2", lambda: obs_all.at[pl.ds(0, 3)]),) * 2
         for d in (1, 2, 3):
             send(obs_all.at[r], obs_all.at[r], dev(dy=d), o_in, o_out)
-        qbuf[q] = (pbuf[0] + pbuf[1]) + (pbuf[2] + pbuf[3])
-        p_in, p_out = (("p2", lambda: qbuf.at[pl.ds(0, 7)]),) * 2
-        for dz, dc in line:
-            send(qbuf.at[q], qbuf.at[q], dev(dz=dz, dc=dc), p_in, p_out)
+        tot[...] = (pbuf[0] + pbuf[1]) + (pbuf[2] + pbuf[3])
+        tbuf[x] = tot[x]
+        p_in, p_out = ("p2", lambda: tbuf.at[pl.ds(0, 3)]), ("p2", lambda: tot.at[pl.ds(0, 3)])
+        for d in (1, 2, 3):
+            send(tot.at[x_of[d]], tbuf.at[x], dev(dx=d), p_in, p_out)
 
     def small3():
         wait(got, "o2")
@@ -353,19 +356,18 @@
         o_in, o_out = (("o3", lambda: obs_all.at[pl.ds(0, 12)]),) * 2
         for d in (1, 2, 3):
             send(obs_all.at[x_rows], obs_all.at[x_rows], dev(dx=d), o_in, o_out)
+        qbuf[q] = (tbuf[0] + tbuf[1]) + (tbuf[2] + tbuf[3])
+        p_in, p_out = (("p3", lambda: qbuf.at[pl.ds(0, 7)]),) * 2
+        for dz, dc in line:
+            send(qbuf.at[q], qbuf.at[q], dev(dz=dz, dc=dc), p_in, p_out)
+
+    def small4():
+        wait(got, "o3")
+        wait(got, "p3")
         total = qbuf[0]
         for i in range(1, 8):
             total = total + qbuf[i]
-        tot[...] = total
-        tbuf[x] = tot[x]
-        p_in, p_out = ("p3", lambda: tbuf.at[pl.ds(0, 3)]), ("p3", lambda: tot.at[pl.ds(0, 3)])
-        for d in (1, 2, 3):
-            send(tot.at[x_of[d]], tbuf.at[x], dev(dx=d), p_in, p_out)
-
-    def small4():
-        wait(got, "o3")
-        wait(got, "p3")
-        rhs[...] = (tbuf[0] + tbuf[1]) + (tbuf[2] + tbuf[3])
+        rhs[...] = total
         every = obs_all[...].reshape(16 * 8, 1, TB)
         block_of = lax.broadcasted_iota(jnp.int32, every.shape, 0)
         bal[...] = jnp.sum(jnp.where(block_of == plan[...], every, 0.0), axis=0)
@@ -403,12 +405,12 @@
     stage_r(3)
     stage_c(3)
     r1(0)
+    spread_r(2)
     c1(0)
     small1()
     r2(0)
     r1(1)
     c2(0)
-    spread_r(2)
     spread_c(2)
     c1(1)
     rd(0)
@@ -522,7 +524,7 @@
             pltpu.VMEM((16, 8, 1, TB), F32),
             pltpu.VMEM((4, 4, 3, TB), F32),
             pltpu.VMEM((4, 4, 3, TB), F32),
-            pltpu.VMEM((8, 4, 3, TB), F32),
+            pltpu.VMEM((8, 3, TB), F32),
             pltpu.VMEM((4, 3, TB), F32),
             pltpu.VMEM((4, 3, TB), F32),
             pltpu.SemaphoreType.DMA,

time: 89.8 us -> 89.8 us (level)
  no operation moved by 1% of the time
where the time goes in v4:
time: 89.8 us; the launch traced here: 89.6 us
  Pallas kernels  88.3 us (98%)
  between operations  1.29 us (1%)
    pallas_call x1, Pallas kernels, on_device(): pl.pallas_call(kernel, name='normal_equations', out_shape=(pltpu.VMEM((38...  87.3 us

profile of v4, /device:TPU:1, one launch (start us, length us, event | category | flops | bytes accessed | tf_op | source)
XLA Modules:
  0.0 89.6 jit_solution(661966532215519847)
XLA Ops:
  1.3 87.3 %normal_equations.1 = (f32[384,768]{1,0:T(8,128)S(1)}, f32[3,128]{1,0:T(4,128)S(1)}, f32[1,128]{1,0:T(1,128)S(1)}) custom-call(s32[48]{0:T(128)} %tile_map.1, s32[1,4]{1,0:T(1,128)} %lens.1, f32[1,4]{1,0:T(1,128)} %amps.1, f32[1,4]{1,0:T(1,128)} %decays.1, s32[1,1]{1,0:T(1,128)} %bitcast.4.plan, bf16[128,6144]{1,0:T(8,128)(2,1)} %design.1, ...), custom_call_target="tpu_custom_call" | custom-call | tf_op jit(solution)/shard_map/normal_equations/pallas_call | solution.py:502
  88.5 1.0 %hand_over.1 = (f32[384,768]{1,0:T(8,128)}, f32[384]{0:T(512)}, f32[1,128]{1,0:T(1,128)}) custom-call(f32[384,768]{1,0:T(8,128)S(1)} %get-tuple-element.6.gram, f32[3,128]{1,0:T(4,128)S(1)} %get-tuple-element.7.rhs, f32[1,128]{1,0:T(1,128)S(1)} %get-tuple-element.8.bal), custom_call_target="tpu_custom_call" | custom-call | tf_op jit(solution)/shard_map/hand_over/pallas_call | solution.py:552

commit v5 on v4

--- a/solution.py
+++ b/solution.py
@@ -102,7 +102,7 @@
     def dev(dx=0, dy=0, dz=0, dc=0):
         return places[dx, dy, dz, dc]
 
-    x_of = [(x + d) % 4 for d in range(4)]
+    y_of = [(y + d) % 4 for d in range(4)]
     x_rows = pl.ds(4 * x, 4)
 
     got, left = {}, {}
@@ -325,18 +325,18 @@
             return carry
 
         lax.fori_loop(0, 24, partial, 0, unroll=6)
-        for dy in range(4):
-            for xx in range(4):
+        for dx in range(4):
+            for yy in range(4):
                 for i in range(3):
-                    t = tile_map[xx * 12 + (y + dy) % 4 * 3 + i]
-                    psend[dy, xx, i : i + 1] = pall[t]
+                    t = tile_map[(x + dx) % 4 * 12 + yy * 3 + i]
+                    psend[dx, yy, i : i + 1] = pall[t]
         o_in, o_out = (("o1", lambda: obs_all.at[r, pl.ds(0, 7)]),) * 2
         for dz, dc in line:
             send(obs_all.at[r, q], obs_all.at[r, q], dev(dz=dz, dc=dc), o_in, o_out)
-        pbuf[y] = psend[0]
+        pbuf[x] = psend[0]
         p_in, p_out = ("p1", lambda: pbuf.at[pl.ds(0, 3)]), ("p1", lambda: psend.at[pl.ds(1, 3)])
         for d in (1, 2, 3):
-            send(psend.at[d], pbuf.at[y], dev(dy=d), p_in, p_out)
+            send(psend.at[d], pbuf.at[x], dev(dx=d), p_in, p_out)
 
     def small2():
         wait(got, "o1")
@@ -345,10 +345,10 @@
         for d in (1, 2, 3):
             send(obs_all.at[r], obs_all.at[r], dev(dy=d), o_in, o_out)
         tot[...] = (pbuf[0] + pbuf[1]) + (pbuf[2] + pbuf[3])
-        tbuf[x] = tot[x]
+        tbuf[y] = tot[y]
         p_in, p_out = ("p2", lambda: tbuf.at[pl.ds(0, 3)]), ("p2", lambda: tot.at[pl.ds(0, 3)])
         for d in (1, 2, 3):
-            send(tot.at[x_of[d]], tbuf.at[x], dev(dx=d), p_in, p_out)
+            send(tot.at[y_of[d]], tbuf.at[y], dev(dy=d), p_in, p_out)
 
     def small3():
         wait(got, "o2")
@@ -404,8 +404,8 @@
     stage_c(2)
     stage_r(3)
     stage_c(3)
+    spread_r(2)
     r1(0)
-    spread_r(2)
     c1(0)
     small1()
     r2(0)
@@ -486,7 +486,8 @@
 def hand_over(gram, rhs, bal, gram_out, rhs_out, bal_out, flat, sem):
     for i in range(3):
         flat[i * TB : (i + 1) * TB] = rhs[i]
-    pairs = ((gram, gram_out), (bal, bal_out), (flat, rhs_out))
+    rows = [pl.ds(i * 96, 96) for i in range(4)]
+    pairs = [(gram.at[part], gram_out.at[part]) for part in rows] + [(bal, bal_out), (flat, rhs_out)]
     copies = [pltpu.make_async_copy(src, dst, sem.at[i]) for i, (src, dst) in enumerate(pairs)]
     for cp in copies:
         cp.start()
@@ -559,7 +560,7 @@
         ),
         in_specs=[vmem] * 3,
         out_specs=(anywhere, anywhere, anywhere),
-        scratch_shapes=[pltpu.VMEM((384,), F32), pltpu.SemaphoreType.DMA((3,))],
+        scratch_shapes=[pltpu.VMEM((384,), F32), pltpu.SemaphoreType.DMA((6,))],
         compiler_params=pltpu.CompilerParams(vmem_limit_bytes=1024 * 1024),
     )(*inner)
 

time: 89.8 us -> 89.6 us (level)
  no operation moved by 1% of the time
where the time goes in v5:
time: 89.6 us; the launch traced here: 89.3 us
  Pallas kernels  88 us (98%)
  between operations  1.29 us (1%)
    pallas_call x1, Pallas kernels, on_device(): pl.pallas_call(kernel, name='normal_equations', out_shape=(pltpu.VMEM((38...  87 us

profile of v5, /device:TPU:1, one launch (start us, length us, event | category | flops | bytes accessed | tf_op | source)
XLA Modules:
  0.0 89.3 jit_solution(4356082603977098125)
XLA Ops:
  1.3 87.0 %normal_equations.1 = (f32[384,768]{1,0:T(8,128)S(1)}, f32[3,128]{1,0:T(4,128)S(1)}, f32[1,128]{1,0:T(1,128)S(1)}) custom-call(s32[48]{0:T(128)} %tile_map.1, s32[1,4]{1,0:T(1,128)} %lens.1, f32[1,4]{1,0:T(1,128)} %amps.1, f32[1,4]{1,0:T(1,128)} %decays.1, s32[1,1]{1,0:T(1,128)} %bitcast.4.plan, bf16[128,6144]{1,0:T(8,128)(2,1)} %design.1, ...), custom_call_target="tpu_custom_call" | custom-call | tf_op jit(solution)/shard_map/normal_equations/pallas_call | solution.py:503
  88.3 1.1 %hand_over.1 = (f32[384,768]{1,0:T(8,128)}, f32[384]{0:T(512)}, f32[1,128]{1,0:T(1,128)}) custom-call(f32[384,768]{1,0:T(8,128)S(1)} %get-tuple-element.6.gram, f32[3,128]{1,0:T(4,128)S(1)} %get-tuple-element.7.rhs, f32[1,128]{1,0:T(1,128)S(1)} %get-tuple-element.8.bal), custom_call_target="tpu_custom_call" | custom-call | tf_op jit(solution)/shard_map/hand_over/pallas_call | solution.py:553

commit v6 on v5

--- a/solution.py
+++ b/solution.py
@@ -42,18 +42,20 @@
     b = jnp.where(start, amp, jnp.where(live_prev, q * noise_prev, q))
     c = jnp.where(start, 0.0, jnp.where(live_prev, 1.0, 0.0))
     d = jnp.where(start, 1.0, jnp.where(live_prev, noise_prev, 1.0))
-    for shift in (1, 2, 4, 8, 16, 32):
-        ok = pos >= shift
-        ap, bp = pltpu.roll(a, shift, 1), pltpu.roll(b, shift, 1)
-        cp, dp = pltpu.roll(c, shift, 1), pltpu.roll(d, shift, 1)
-        an = jnp.where(ok, a * ap + b * cp, a)
-        bn = jnp.where(ok, a * bp + b * dp, b)
-        cn = jnp.where(ok, c * ap + d * cp, c)
-        dn = jnp.where(ok, c * bp + d * dp, d)
-        if shift == 8:
-            scale = 1.0 / (an + bn + cn + dn)
-            an, bn, cn, dn = an * scale, bn * scale, cn * scale, dn * scale
-        a, b, c, d = an, bn, cn, dn
+    for shift in (1, 4, 16):
+        whole = (a, b, c, d)
+        for n in (1, 2, 3):
+            ok = pos >= n * shift
+            ap, bp, cp, dp = (pltpu.roll(v, n * shift, 1) for v in whole)
+            a, b, c, d = (
+                jnp.where(ok, a * ap + b * cp, a),
+                jnp.where(ok, a * bp + b * dp, b),
+                jnp.where(ok, c * ap + d * cp, c),
+                jnp.where(ok, c * bp + d * dp, d),
+            )
+        if shift == 4:
+            scale = 1.0 / (a + b + c + d)
+            a, b, c, d = a * scale, b * scale, c * scale, d * scale
     var = b / d
     is_live = live > 0.5
     total = jnp.where(is_live, var, 0.0) + noise
@@ -84,10 +86,10 @@
 
 
 def kernel(
-    tile_map, lens, amps, decays, plan, design, obs, gaps, noise,
+    tile_map_in, lens_in, amps_in, decays_in, plan_in, design, obs_in, gaps_in, noise_in,
     gram, rhs, bal,
-    dbuf, wn, wt, pall, rbuf, rsend, cbuf, csend, own, rss, rsr, obs_all, psend, pbuf, qbuf, tot, tbuf,
-    load_sem, ssem, rsem, sum_ssem, sum_rsem,
+    tile_map, lens, amps, decays, plan, obs, gaps, noise, dbuf, wn, wt, pall, rbuf, rsend, cbuf, csend, own, rss, rsr, obs_all, psend, pbuf, qbuf, tot, tbuf,
+    in_sem, load_sem, ssem, rsem, sum_ssem, sum_rsem,
 ):
     r, q = lax.axis_index("row"), lax.axis_index("col")
     x, y, z, c = r // 4, r % 4, q // 2, q % 2
@@ -122,6 +124,11 @@
             device_id=to, device_id_type=MESH,
         ).start()
 
+    first = ((lens_in, lens), (amps_in, amps), (decays_in, decays), (gaps_in, gaps), (noise_in, noise), (obs_in, obs))
+    pairs = first + ((tile_map_in, tile_map), (plan_in, plan))
+    loads = [pltpu.make_async_copy(src, dst, in_sem.at[i]) for i, (src, dst) in enumerate(pairs)]
+    for cp in loads:
+        cp.start()
     for t in range(48):
         pltpu.make_async_copy(design.at[:, pl.ds(t * TB, TB)], dbuf.at[t], load_sem).start()
     line = [(dz, dc) for dz in range(4) for dc in range(2) if (dz, dc) != (0, 0)]
@@ -129,6 +136,8 @@
     for p in places.values():
         pl.semaphore_signal(barrier, inc=1, device_id=p, device_id_type=MESH)
 
+    for cp in loads:
+        cp.wait()
     inv, white_row = inverse_factor(lens, amps, decays, gaps[...], noise[...], obs[...])
     hi = inv.astype(BF16)
     lo = (inv - hi.astype(F32)).astype(BF16)
@@ -277,34 +286,37 @@
         k, j, j2 = (pick(s, [block[i] for block in ORDER]) for i in range(3))
         groups = [(rz, rc, ry) for rz in range(4) for rc in range(2) for ry in range(4)]
         lhs = jnp.concatenate([rbuf[k, rz, rc, ry] for rz, rc, ry in groups], axis=1)
-        left = jnp.concatenate([cbuf[j, ry, rz * 2 + rc] for rz, rc, ry in groups], axis=0)
-        right = jnp.concatenate([cbuf[j2, ry, rz * 2 + rc] for rz, rc, ry in groups], axis=0)
+        early = (j == NJ - 1) & (j2 == NJ - 1)
+        far, far2 = jnp.where(early, NJ, j), jnp.where(early, NJ, j2)
+        left = jnp.concatenate([cbuf[far if ry == 2 else j, ry, rz * 2 + rc] for rz, rc, ry in groups], axis=0)
+        right = jnp.concatenate([cbuf[far2 if ry == 2 else j2, ry, rz * 2 + rc] for rz, rc, ry in groups], axis=0)
         value = jnp.dot(lhs, jnp.concatenate([left, right], axis=1), preferred_element_type=F32)
         last = k == NA - 1
-        own[jnp.where(last, j, NJ)] = value[:, :TB]
+        own[jnp.where(last, j, jnp.where(early, NJ + 1 + k, NJ))] = value[:, :TB]
         own[jnp.where(last, j2, NJ)] = value[:, TB:]
         rss[j, k] = value[:, :TB].astype(BF16)
         rss[j2, k] = value[:, TB:].astype(BF16)
 
+        pl.when(jnp.logical_not(early))(lambda: reduce_tile(j, k))
+        pl.when(j2 > j)(lambda: reduce_tile(j2, k))
+
+    def late(k, carry):
+        lhs = jnp.concatenate([rbuf[k, rz, rc, 2] for rz in range(4) for rc in range(2)], axis=1)
+        right = jnp.concatenate([cbuf[NJ - 1, 2, i] for i in range(8)], axis=0)
+        value = own[NJ + 1 + k] + jnp.dot(lhs, right, preferred_element_type=F32)
+        rss[NJ - 1, k] = value.astype(BF16)
+        reduce_tile(NJ - 1, k)
+        return carry
+
+    def reduce_tile(j, k):
         @pl.when(k == 0)
         def _():
-            to = place(2, 0, 0, 0)
-            reduce(j, k, 0, to).start()
-
-            @pl.when(j2 > j)
-            def _():
-                reduce(j2, k, 0, to).start()
+            reduce(j, k, 0, place(2, 0, 0, 0)).start()
 
         @pl.when((k == 1) | (k == 2))
         def _():
-            up, dn = place(1, 0, 0, 0), place(3, 0, 0, 0)
-            reduce(j, k, 1, up).start()
-            reduce(j, k, 3, dn).start()
-
-            @pl.when(j2 > j)
-            def _():
-                reduce(j2, k, 1, up).start()
-                reduce(j2, k, 3, dn).start()
+            reduce(j, k, 1, place(1, 0, 0, 0)).start()
+            reduce(j, k, 3, place(3, 0, 0, 0)).start()
 
     def reduce(j, k, dx, to):
         if dx == 0:
@@ -405,6 +417,7 @@
     stage_r(3)
     stage_c(3)
     spread_r(2)
+    cbuf[NJ, 2] = jnp.zeros((8, TB, TB), BF16)
     r1(0)
     c1(0)
     small1()
@@ -452,14 +465,18 @@
 
     def before9():
         small3()
+        wait(got, "crest3")
+
+    def before11():
         re(3)
-        cf(3)
 
     def before12():
+        wait(got, "cfar3")
+        lax.fori_loop(0, 3, late, 0)
         rf(3)
 
     acts = (
-        (1, before1), (2, before2), (4, before4), (6, before6), (8, before8), (9, before9), (12, before12),
+        (1, before1), (2, before2), (4, before4), (6, before6), (8, before8), (9, before9), (11, before11), (12, before12),
     )
 
     def slot(s, carry):
@@ -498,7 +515,6 @@
 def on_device(
     design, observations, gaps, noise_var, arc_lengths, arc_amp, arc_decay, plan, tile_map
 ):
-    smem = pl.BlockSpec(memory_space=pltpu.SMEM)
     vmem = pl.BlockSpec(memory_space=pltpu.VMEM)
     gram, rhs, bal = pl.pallas_call(
         kernel,
@@ -508,18 +524,26 @@
             pltpu.VMEM((3, TB), F32),
             pltpu.VMEM((1, TB), F32),
         ),
-        in_specs=[smem] * 4 + [vmem, pl.BlockSpec(memory_space=pl.ANY)] + [vmem] * 3,
+        in_specs=[pl.BlockSpec(memory_space=pl.ANY)] * 9,
         out_specs=(vmem, vmem, vmem),
         scratch_shapes=[
+            pltpu.SMEM((48,), jnp.int32),
+            pltpu.SMEM((1, 4), jnp.int32),
+            pltpu.SMEM((1, 4), F32),
+            pltpu.SMEM((1, 4), F32),
+            pltpu.VMEM((1, 1), jnp.int32),
+            pltpu.VMEM((1, TB), F32),
+            pltpu.VMEM((1, TB), jnp.int32),
+            pltpu.VMEM((1, TB), F32),
             pltpu.VMEM((48, TB, TB), BF16),
             pltpu.VMEM((48, TB, TB), BF16),
             pltpu.VMEM((48, TB, TB), BF16),
             pltpu.VMEM((48, 1, TB), F32),
             pltpu.VMEM((NA, 4, 2, 4, 384, TB), BF16),
             pltpu.VMEM((NA, 3, 384, TB), BF16),
-            pltpu.VMEM((NJ, 4, 8, TB, TB), BF16),
+            pltpu.VMEM((NJ + 1, 4, 8, TB, TB), BF16),
             pltpu.VMEM((NJ, 7, TB, TB), BF16),
-            pltpu.VMEM((NJ + 1, 384, TB), F32),
+            pltpu.VMEM((NJ + 4, 384, TB), F32),
             pltpu.VMEM((NJ, 4, 384, TB), BF16),
             pltpu.VMEM((NJ, 4, 384, TB), BF16),
             pltpu.VMEM((16, 8, 1, TB), F32),
@@ -528,6 +552,7 @@
             pltpu.VMEM((8, 3, TB), F32),
             pltpu.VMEM((4, 3, TB), F32),
             pltpu.VMEM((4, 3, TB), F32),
+            pltpu.SemaphoreType.DMA((8,)),
             pltpu.SemaphoreType.DMA,
             pltpu.SemaphoreType.DMA((N_LEFT,)),
             pltpu.SemaphoreType.DMA((N_GOT,)),

time: 89.6 us -> 88.7 us (0.990)
  no operation moved by 1% of the time
where the time goes in v6:
time: 88.7 us; the launch traced here: 88.5 us
  Pallas kernels  87.2 us (98%)
  between operations  1.29 us (1%)
    pallas_call x1, Pallas kernels, on_device(): pl.pallas_call(kernel, name='normal_equations', out_shape=(pltpu.VMEM((38...  86.2 us

profile of v6, /device:TPU:1, one launch (start us, length us, event | category | flops | bytes accessed | tf_op | source)
XLA Modules:
  0.0 88.5 jit_solution(4616445239571440631)
XLA Ops:
  1.3 86.2 %normal_equations.1 = (f32[384,768]{1,0:T(8,128)S(1)}, f32[3,128]{1,0:T(4,128)S(1)}, f32[1,128]{1,0:T(1,128)S(1)}) custom-call(s32[48]{0:T(128)} %tile_map_in.1, s32[1,4]{1,0:T(1,128)} %lens_in.1, f32[1,4]{1,0:T(1,128)} %amps_in.1, f32[1,4]{1,0:T(1,128)} %decays_in.1, s32[1,1]{1,0:T(1,128)} %bitcast.4.plan_in, bf16[128,6144]{1,0:T(8,128)(2,1)} %design.1, ...), custom_call_target="tpu_custom_call" | custom-call | tf_op jit(solution)/shard_map/normal_equations/pallas_call | solution.py:519
  87.5 1.1 %hand_over.1 = (f32[384,768]{1,0:T(8,128)}, f32[384]{0:T(512)}, f32[1,128]{1,0:T(1,128)}) custom-call(f32[384,768]{1,0:T(8,128)S(1)} %get-tuple-element.6.gram, f32[3,128]{1,0:T(4,128)S(1)} %get-tuple-element.7.rhs, f32[1,128]{1,0:T(1,128)S(1)} %get-tuple-element.8.bal), custom_call_target="tpu_custom_call" | custom-call | tf_op jit(solution)/shard_map/hand_over/pallas_call | solution.py:578

commit v7 on v6

--- a/solution.py
+++ b/solution.py
@@ -16,7 +16,7 @@
     (0, 0, 1), (1, 0, 1), (0, 2, 3), (1, 2, 3), (2, 0, 1), (2, 2, 3), (0, 4, 4), (1, 4, 4), (2, 4, 4),
     (0, 5, 5), (1, 5, 5), (2, 5, 5), (3, 0, 1), (3, 2, 3), (3, 4, 5),
 )
-N_GOT, N_LEFT = 50, 13
+N_GOT, N_LEFT = 47, 13
 
 
 def inverse_factor(lens, amps, decays, gaps, noise, obs):
@@ -220,11 +220,16 @@
     def pieces(part):
         return [pl.ds(i, 1) for i in range(part.start, part.start + part.size)]
 
+    def c_both(b):
+        return (f"cboth{b}", lambda: cbuf.at[tiles(b), pl.ds(1, 2)])
+
     def gather1(ref, i, up, dn, halves, name, leaving):
         first, second = halves
         wait(got, f"{name}{i}")
         one, other = (f"{name}up{i}", lambda: ref(i, 3, first)), (f"{name}dn{i}", lambda: ref(i, 1, second))
         rest = (f"{name}rest{i}", lambda: ref(i, 1, pl.ds(0, 2 * first.size)))
+        if name == "c" and i < NB - 1:
+            rest = c_both(i)
         for p, p2 in zip(pieces(first), pieces(second)):
             send(ref(i, 0, p), ref(i, 3, p), up, one, leaving)
             send(ref(i, 0, p2), ref(i, 1, p2), dn, other, leaving)
@@ -234,6 +239,8 @@
     def gather2(ref, i, up, dn, halves, name, leaving):
         first, second = halves
         far = (f"{name}far{i}", lambda: ref(i, 2, pl.ds(0, 2 * first.size)))
+        if name == "c" and i < NB - 1:
+            far = c_both(i)
         wait(got, f"{name}up{i}")
         for p in pieces(first):
             send(ref(i, 3, p), ref(i, 2, p), up, far, leaving)
@@ -273,8 +280,7 @@
         gather2(c_ref, b, y_up, y_dn, c_halves, "c", c2_left)
 
     def cf(b):
-        wait(got, f"crest{b}")
-        wait(got, f"cfar{b}")
+        wait(got, f"cboth{b}")
 
     def pick(s, values):
         out = values[0]
@@ -325,7 +331,7 @@
             src = rss.at[j, k, pl.ds(192 * (dx // 2), 192)]
             dst = rsr.at[j, 4 - dx, pl.ds((k - 1) * 192, 192)]
         return pltpu.make_async_remote_copy(
-            src_ref=src, dst_ref=dst, send_sem=sum_ssem, recv_sem=sum_rsem.at[j],
+            src_ref=src, dst_ref=dst, send_sem=sum_ssem, recv_sem=sum_rsem.at[jnp.where(j == NJ - 1, 1, 0)],
             device_id=to, device_id_type=MESH,
         )
 
@@ -417,6 +423,7 @@
     stage_r(3)
     stage_c(3)
     spread_r(2)
+    spread_c(2)
     cbuf[NJ, 2] = jnp.zeros((8, TB, TB), BF16)
     r1(0)
     c1(0)
@@ -424,7 +431,6 @@
     r2(0)
     r1(1)
     c2(0)
-    spread_c(2)
     c1(1)
     rd(0)
     re(0)
@@ -488,8 +494,9 @@
     lax.fori_loop(0, len(ORDER), slot, 0)
     small4()
     for j in range(NJ):
-        arrived = rsr.at[j, pl.ds(1, 3)]
-        pltpu.make_async_copy(arrived, arrived, sum_rsem.at[j]).wait()
+        if j == 0 or j == NJ - 1:
+            arrived = rsr.at[pl.ds(0, NJ - 1) if j == 0 else NJ - 1, pl.ds(1, 3)]
+            pltpu.make_async_copy(arrived, arrived, sum_rsem.at[j // (NJ - 1)]).wait()
         total = own[j]
         for dx in (1, 2, 3):
             total = total + rsr[j, dx].astype(F32)
@@ -557,7 +564,7 @@
             pltpu.SemaphoreType.DMA((N_LEFT,)),
             pltpu.SemaphoreType.DMA((N_GOT,)),
             pltpu.SemaphoreType.DMA,
-            pltpu.SemaphoreType.DMA((NJ,)),
+            pltpu.SemaphoreType.DMA((2,)),
         ],
         compiler_params=pltpu.CompilerParams(
             collective_id=0, has_side_effects=True, vmem_limit_bytes=60 * 1024 * 1024

time: 88.7 us -> 88.7 us (level)
  no operation moved by 1% of the time
where the time goes in v7:
time: 88.7 us; the launch traced here: 88.5 us
  Pallas kernels  87.2 us (98%)
  between operations  1.29 us (1%)
    pallas_call x1, Pallas kernels, on_device(): pl.pallas_call(kernel, name='normal_equations', out_shape=(pltpu.VMEM((38...  86.1 us

profile of v7, /device:TPU:1, one launch (start us, length us, event | category | flops | bytes accessed | tf_op | source)
XLA Modules:
  0.0 88.5 jit_solution(4141114846662844234)
XLA Ops:
  1.3 86.1 %normal_equations.1 = (f32[384,768]{1,0:T(8,128)S(1)}, f32[3,128]{1,0:T(4,128)S(1)}, f32[1,128]{1,0:T(1,128)S(1)}) custom-call(s32[48]{0:T(128)} %tile_map_in.1, s32[1,4]{1,0:T(1,128)} %lens_in.1, f32[1,4]{1,0:T(1,128)} %amps_in.1, f32[1,4]{1,0:T(1,128)} %decays_in.1, s32[1,1]{1,0:T(1,128)} %bitcast.4.plan_in, bf16[128,6144]{1,0:T(8,128)(2,1)} %design.1, ...), custom_call_target="tpu_custom_call" | custom-call | tf_op jit(solution)/shard_map/normal_equations/pallas_call | solution.py:526
  87.4 1.1 %hand_over.1 = (f32[384,768]{1,0:T(8,128)}, f32[384]{0:T(512)}, f32[1,128]{1,0:T(1,128)}) custom-call(f32[384,768]{1,0:T(8,128)S(1)} %get-tuple-element.6.gram, f32[3,128]{1,0:T(4,128)S(1)} %get-tuple-element.7.rhs, f32[1,128]{1,0:T(1,128)S(1)} %get-tuple-element.8.bal), custom_call_target="tpu_custom_call" | custom-call | tf_op jit(solution)/shard_map/hand_over/pallas_call | solution.py:585
